TPU v7x, 128 devices: a whole 4x4x4 slice. The times are simulated.
128 devices in a mesh: dp: 4 (over x), vocab: 32 (over y, z, core).
Axes of the slice: x: 4, y: 4, z: 4, core: 2. Of those that a mesh axis runs over, the one named last changes fastest.
Arguments:
- hidden: bfloat16 [1024, 5120], P('dp')
- head_t: bfloat16 [5120, 77824], P('dp', 'vocab'), may hold values from -0.25 to 0.25
- targets: int32 [1024], P('dp'), may hold values from 0 to 77823
- token_ids: int32 [1024], P('dp'), may hold values from 0 to 77823, as said below
- embed_cot: bfloat16 [1024, 5120], P('dp'), may hold values from -6 to 6
Outputs:
- head_grad: bfloat16 [5120, 77824], P('dp', 'vocab')
- embed_grad: bfloat16 [5120, 77824], P('dp', 'vocab')
- hidden_grad: bfloat16 [1024, 5120], P('vocab', 'dp')
Inputs may be any that keep to these rules, and one draw needn't show every extreme that they name: `token_ids`: among the 256 input ids of one data group, at most 16 lie in any one block of 2432 vocabulary rows that starts at a multiple of 2432; in every group some block holds exactly 16.
All inputs are finite; a program needn't handle non-finite values.
Results may differ from a plain program's by a relative error of at most 0.0033.
Values may be sent and summed in bfloat16 or wider, within the bound.
No kernel may reach another device: no remote copies, remote signals or barrier semaphores. Data moves between devices by JAX's collectives and lax.ppermute only.
A program may use at most 128 MiB of HBM per device.

v0:
```python
import jax
import jax.numpy as jnp
from jax import lax
from jax.experimental import pallas as pl
from jax.experimental.pallas import tpu as pltpu
from jax.sharding import PartitionSpec as P


LANES = 128
BF = jnp.bfloat16
F32 = jnp.float32


def shift_x(a, s):
    n = lax.axis_size("dp")
    return lax.ppermute(a, "dp", [(i, (i + s) % n) for i in range(n)])


def vocab_perm(dy, dz, dc):
    pairs = []
    for v in range(32):
        y, z, c = v // 8, (v // 2) % 4, v % 2
        pairs.append((v, ((y + dy) % 4) * 8 + ((z + dz) % 4) * 2 + (c + dc) % 2))
    return pairs


def shift_v(a, dy, dz, dc):
    return lax.ppermute(a, "vocab", vocab_perm(dy, dz, dc))


def vmem(mib):
    return pltpu.CompilerParams(vmem_limit_bytes=mib * 2**20)


def pack_kernel(offs, *refs):
    n = len(refs) // 2
    for src, dst in zip(refs[:n], refs[n:]):
        dst[...] = src[...]


def pack(head_t, offs, tiles):
    rows, n = head_t.shape[0], offs.shape[0]

    def at(s):
        return lambda t, o: (0, o[s] + t)

    return pl.pallas_call(
        pack_kernel,
        grid_spec=pltpu.PrefetchScalarGridSpec(
            num_scalar_prefetch=1,
            grid=(tiles,),
            in_specs=[pl.BlockSpec((rows, LANES), at(s)) for s in range(n)],
            out_specs=[pl.BlockSpec((rows, LANES), lambda t, o: (0, t))] * n,
        ),
        out_shape=[jax.ShapeDtypeStruct((rows, tiles * LANES), BF)] * n,
        compiler_params=vmem(6),
        name="pack",
    )(offs, *([head_t] * n))


def assemble_kernel(at, p0, p1, p2, p3, left, right):
    depth = left.shape[-1] // 2
    for s, p in enumerate((p0, p1, p2, p3)):
        j = at[s]
        for dst, first, second in ((left, 0, 3), (right, 1, 2)):
            for i, slot in enumerate((first, second)):
                start = pl.multiple_of(at[slot] * depth, depth)
                dst[j, :, i * depth : (i + 1) * depth] = p[:, pl.ds(start, depth)]
        right[j, :, 2 * depth :] = p[:, 4 * depth :]


def assemble(at, parts, depth):
    rows = parts[0].shape[0]
    whole = lambda shape: pl.BlockSpec(shape, lambda i, at: (0,) * len(shape))
    shapes = [(4, rows, 2 * depth), (4, rows, 2 * depth + LANES)]
    return pl.pallas_call(
        assemble_kernel,
        grid_spec=pltpu.PrefetchScalarGridSpec(
            num_scalar_prefetch=1,
            grid=(1,),
            in_specs=[whole(parts[0].shape)] * 4,
            out_specs=[whole(s) for s in shapes],
        ),
        out_shape=[jax.ShapeDtypeStruct(s, BF) for s in shapes],
        compiler_params=vmem(8),
        name="assemble",
    )(at, *parts)


def add_products(total, pairs, weights):
    half = pairs[0][0].shape[0]
    for i in range(2):
        part = None
        for pair, w in zip(pairs, weights):
            new = jnp.dot(pair[i][...], w[...], preferred_element_type=F32)
            part = new if part is None else part + new
        total[i * half : (i + 1) * half, :] += part


def first_kernel(own1, oth1, own2, oth2, w1, w2, out):
    @pl.when(pl.program_id(0) == 0)
    def _():
        out[...] = jnp.zeros_like(out)

    add_products(out, ((own1, oth1), (own2, oth2)), (w1, w2))


def mid_kernel(own, oth, w, acc, out):
    @pl.when(pl.program_id(0) == 0)
    def _():
        out[...] = acc[...]

    add_products(out, ((own, oth),), (w,))


def strips(half, step, start):
    spec = lambda: pl.BlockSpec((half, step), lambda t, *q: (0, t + start))
    return [spec(), spec()]


def partial_logits(kernel, sources, weights, acc, step):
    depth, width = weights[0].shape
    steps = depth // step
    half = sources[0][0].shape[0]
    specs, args = [], []
    for own, oth, start in sources:
        specs += strips(half, step, start * steps)
        args += [own, oth]
    specs += [pl.BlockSpec((step, width), lambda t: (t, 0))] * len(weights)
    args += weights
    whole = pl.BlockSpec((2 * half, width), lambda t: (0, 0))
    if acc is not None:
        specs.append(whole)
        args.append(acc)
    return pl.pallas_call(
        kernel,
        grid=(steps,),
        in_specs=specs,
        out_specs=whole,
        out_shape=jax.ShapeDtypeStruct((2 * half, width), F32),
        cost_estimate=pl.CostEstimate(
            flops=4 * half * depth * width * len(weights),
            bytes_accessed=6_000_000 * len(weights),
            transcendentals=0,
        ),
        compiler_params=vmem(20),
    )(*args)


def rows_of(q, k, piece):
    part = piece // 4
    sy = lax.rem(k + 4 - q[0], 4) * piece
    return [(pl.multiple_of(sy + lax.rem(i + 4 - q[4], 4) * part, part), part) for i in range(4)]


def last_kernel(q, own, oth, dig_own, dig_oth, w, acc, *rest):
    *e_outs, st_out, total = rest
    t = pl.program_id(0)

    @pl.when(t == 0)
    def _():
        total[...] = acc[...]

    add_products(total, ((own, oth),), (w,))

    @pl.when(t == pl.num_programs(0) - 1)
    def _():
        half = own.shape[0]
        piece = half // 4
        per = 4 // len(e_outs)
        for k in range(4):
            for sc in range(2):
                near = q[5] == sc
                spots = rows_of(q, k, piece)
                first = jnp.where(near, 0, half)
                logits = jnp.concatenate([total[pl.ds(first + a, b), :] for a, b in spots])
                digits = jnp.where(
                    near,
                    jnp.concatenate([dig_own[pl.ds(a, b), :] for a, b in spots]).astype(F32),
                    jnp.concatenate([dig_oth[pl.ds(a, b), :] for a, b in spots]).astype(F32),
                )
                target = (
                    digits[:, 0:1] * 65536.0 + digits[:, 1:2] * 256.0 + digits[:, 2:3]
                ).astype(jnp.int32) - q[3]
                top = jnp.max(logits, axis=1, keepdims=True)
                expo = jnp.exp(logits - top)
                col = lax.broadcasted_iota(jnp.int32, logits.shape, 1)
                mine = col < q[1]
                count = jnp.sum(jnp.where(mine, expo, 0.0), axis=1, keepdims=True)
                hit = (col + q[2] == target) & mine
                at_target = jnp.sum(jnp.where(hit, logits, 0.0), axis=1, keepdims=True)
                to = (2 * (k % per) + sc) * piece
                e_outs[k // per][to : to + piece, :] = expo.astype(BF)
                lane = lax.broadcasted_iota(jnp.int32, (piece, LANES), 1)
                st_out[(2 * k + sc) * piece : (2 * k + sc + 1) * piece, :] = jnp.where(
                    lane == 0,
                    top,
                    jnp.where(
                        lane == 1, count, jnp.where(lane == 2, at_target, target.astype(F32))
                    ),
                )


def logits_last(q, own, oth, w, acc, step, chunks):
    depth, width = w.shape
    half = own.shape[0]
    steps = depth // step
    rows = 2 * half
    weight = pl.BlockSpec((step, width), lambda t, q: (t, 0))
    digits = pl.BlockSpec((half, LANES), lambda t, q: (0, 2 * depth // LANES))
    const = lambda s: pl.BlockSpec(s, lambda t, q: (0, 0))
    e_shape = (rows // chunks, width)
    return pl.pallas_call(
        last_kernel,
        grid_spec=pltpu.PrefetchScalarGridSpec(
            num_scalar_prefetch=1,
            grid=(steps,),
            in_specs=strips(half, step, steps)
            + [digits, digits, weight, const((rows, width))],
            out_specs=[const(e_shape)] * chunks + [const((rows, LANES))],
            scratch_shapes=[pltpu.VMEM((rows, width), F32)],
        ),
        out_shape=[jax.ShapeDtypeStruct(e_shape, BF)] * chunks
        + [jax.ShapeDtypeStruct((rows, LANES), F32)],
        cost_estimate=pl.CostEstimate(
            flops=8 * half * depth * width, bytes_accessed=14_000_000, transcendentals=0
        ),
        compiler_params=vmem(24),
        name="logits_last",
    )(q, own, oth, own, oth, w, acc)


def transpose_kernel(q, own, oth, out):
    piece = own.shape[0] // 4
    for k in range(4):
        spots = rows_of(q, k, piece)
        near, far = (
            jnp.concatenate([src[pl.ds(a, b), :] for a, b in spots]).astype(F32)
            for src in (own, oth)
        )
        for sc in range(2):
            to = (2 * k + sc) * piece
            block = jnp.where(q[5] == sc, near, far)
            out[:, to : to + piece] = block.T.astype(BF)


def transposed(q, own, oth, depth, block):
    half = own.shape[0]
    source = pl.BlockSpec((half, block), lambda t, q: (0, t))
    return pl.pallas_call(
        transpose_kernel,
        grid_spec=pltpu.PrefetchScalarGridSpec(
            num_scalar_prefetch=1,
            grid=(depth // block,),
            in_specs=[source, source],
            out_specs=pl.BlockSpec((block, 2 * half), lambda t, q: (t, 0)),
        ),
        out_shape=jax.ShapeDtypeStruct((depth, 2 * half), BF),
        cost_estimate=pl.CostEstimate(
            flops=4_000_000, bytes_accessed=5_000_000, transcendentals=0
        ),
        compiler_params=vmem(10),
        name="transposed",
    )(q, own, oth)


def grad_kernel(offs, own, nxt, top, low, prev, coef, stats, head, grads, keep, send):
    rows = own.shape[0]
    half = rows // 2

    @pl.when(pl.program_id(0) == 0)
    def _():
        for h in range(2):
            at = pl.ds(h * half, half)
            across = (top, low)[h][...]
            target = stats[at, 3:4].astype(jnp.int32)
            for s, e in enumerate((own[at, :], nxt[at, :], across, prev[at, :])):
                start = pl.multiple_of(offs[s] * LANES, LANES)
                col = lax.broadcasted_iota(jnp.int32, e.shape, 1)
                prob = e.astype(F32) * coef[at, s : s + 1]
                grad = jnp.where(col == target - start, coef[at, 4:5], prob)
                grads[at, pl.ds(start, e.shape[1])] = grad.astype(BF)

    part = lax.dot_general(
        grads[...], head[...], (((1,), (1,)), ((), ())), preferred_element_type=F32
    )
    piece = rows // 4
    for i in range(2):
        for r in range(0, piece, 8):
            plane = lax.rem(r // 8 % 4 + 4 - offs[4], 4)
            level = lax.rem(r // 32 + 4 - offs[5], 4)
            to = pl.ds(pl.multiple_of(i * piece + level * 32 + plane * 8, 8), 8)
            at = 2 * i * piece + r
            north, south = part[at : at + 8], part[at + piece : at + piece + 8]
            keep[to, :] = jnp.where(offs[6] == 0, north, south)
            send[to, :] = jnp.where(offs[6] == 0, south, north)


def grads_of(offs, es, coef, stats, head_t, chunk, block):
    own, _, _, _, _ = es
    rows, _ = own.shape
    depth, width_dev = head_t.shape
    const = lambda a, i=0: pl.BlockSpec(a, lambda t, o: (i, 0))
    strip = pl.BlockSpec((rows // 2, block), lambda t, o: (0, t))
    return pl.pallas_call(
        grad_kernel,
        grid_spec=pltpu.PrefetchScalarGridSpec(
            num_scalar_prefetch=1,
            grid=(depth // block,),
            in_specs=[const(e.shape) for e in es]
            + [const((rows, LANES), chunk), const((rows, LANES), chunk)]
            + [pl.BlockSpec((block, width_dev), lambda t, o: (t, 0))],
            out_specs=[const((rows, width_dev)), strip, strip],
        ),
        out_shape=[
            jax.ShapeDtypeStruct((rows, width_dev), BF),
            jax.ShapeDtypeStruct((rows // 2, depth), F32),
            jax.ShapeDtypeStruct((rows // 2, depth), F32),
        ],
        cost_estimate=pl.CostEstimate(
            flops=2 * rows * width_dev * depth, bytes_accessed=15_000_000, transcendentals=0
        ),
        compiler_params=vmem(26),
        name="grads",
    )(offs, *es, coef, stats, head_t)


def head_kernel(ht, *refs):
    grads, out = refs[:-1], refs[-1]
    total = None
    at = 0
    for g in grads:
        depth = g.shape[0]
        part = jnp.dot(ht[:, at : at + depth], g[...], preferred_element_type=F32)
        total = part if total is None else total + part
        at += depth
    out[...] = total.astype(BF)


def head_grad_of(ht, grads, block):
    rows, depth = ht.shape
    width = grads[0].shape[1]
    return pl.pallas_call(
        head_kernel,
        grid=(pl.cdiv(width, block),),
        in_specs=[pl.BlockSpec((rows, depth), lambda i: (0, 0))]
        + [pl.BlockSpec((g.shape[0], block), lambda i: (0, i)) for g in grads],
        out_specs=pl.BlockSpec((rows, block), lambda i: (0, i)),
        out_shape=jax.ShapeDtypeStruct((rows, width), BF),
        cost_estimate=pl.CostEstimate(
            flops=2 * rows * depth * width, bytes_accessed=16_000_000, transcendentals=0
        ),
        compiler_params=vmem(26),
        name="head_grad",
    )(ht, *grads)


def everywhere(a, order=(1, 3, 2)):
    got = {0: a}
    for s in order:
        got[s] = shift_x(a, -s)
    return [got[s] for s in range(4)]


def around(a, axis):
    got = {}
    for s in (1, 3, 2):
        got[s] = shift_v(a, -s, 0, 0) if axis == 0 else shift_v(a, 0, -s, 0)
    return [a] + [got[s] for s in (1, 2, 3)]


def over_cores(keep, send):
    got = shift_v(send, 0, 0, 1)
    return keep + got


def scatter_tokens(mine):
    depth = mine.shape[-1]
    mine = mine.reshape(-1, 4, 4, 8, depth)
    parts = []
    for j in (1, 3, 2):
        parts.append(shift_v(mine[:, :, j], j, 0, 0))
    mine = mine[:, :, 0] + parts[0] + parts[1] + parts[2]
    parts = []
    for j in (1, 3, 2):
        parts.append(shift_v(mine[:, j], 0, j, 0))
    mine = mine[:, 0] + parts[0] + parts[1] + parts[2]
    return mine.reshape(-1, depth)


def step(hidden, head_t, targets, token_ids, embed_cot):
    x, v = lax.axis_index("dp"), lax.axis_index("vocab")
    y, z, c = v // 8, (v // 2) % 4, v % 2
    depth, width_dev = head_t.shape
    group = hidden.shape[0]
    planes = lax.axis_size("dp")
    tokens = group * planes
    tiles_dev = width_dev // LANES
    tiles = -(-tiles_dev // planes)
    width = tiles * LANES
    base = v * width_dev
    chunks = 2
    rows = tokens // chunks

    def off(q):
        return jnp.minimum(q * tiles, tiles_dev - tiles)

    slot_plane = [(x + s) % planes for s in range(planes)]
    offs = jnp.stack([off(q) for q in slot_plane]).astype(jnp.int32)

    row = 32 * (v % 8) + 8 * (v // 8)
    tgt = lax.dynamic_slice_in_dim(targets, row, 8)[:, None]
    ids = token_ids.reshape(8, group // 8)

    def base_256(a):
        return [a // 65536, (a // 256) % 256, a % 256]

    digits = jnp.concatenate(
        [*base_256(tgt), jnp.zeros((8, LANES - 3 - 3 * ids.shape[1]), jnp.int32), *base_256(ids)],
        axis=1,
    ).astype(BF)
    rows_mine = lax.dynamic_slice_in_dim(hidden, row, 8, axis=0)
    row_parts = everywhere(jnp.concatenate([rows_mine, digits], axis=1))
    moved = {}
    for s in (1, 3, 2):
        (block,) = pack(head_t, offs[s : s + 1], tiles)
        moved[s] = shift_x(block, s)
    w_prev, w_across, w_next = moved[1], moved[2], moved[3]

    at = jnp.stack(slot_plane).astype(jnp.int32)
    left, right = assemble(at, row_parts, depth)
    left = left.reshape(32, -1)
    right = right.reshape(32, -1)
    left = jnp.concatenate(around(left, 0))
    right = jnp.concatenate(around(right, 1))
    left = jnp.stack([a.reshape(4, 32, -1) for a in around(left, 1)], axis=1)
    left = left.reshape(tokens // 2, -1)
    right = jnp.concatenate(around(right, 0))
    left_oth = shift_v(left, 0, 0, 1)
    right_oth = shift_v(right, 0, 0, 1)

    bound = 2 * group // lax.axis_size("vocab")
    slot_numbers = jnp.arange(bound, dtype=jnp.int32)

    def compact(ids):
        inside = (ids >= base) & (ids < base + width_dev)
        rank = jnp.cumsum(inside.astype(jnp.int32)) - 1
        return (rank[None, :] == slot_numbers[:, None]) & inside[None, :]

    id_digits = jnp.stack([p[:, planes * depth + LANES - 3 * ids.shape[1] :] for p in row_parts])
    d = id_digits.astype(jnp.int32).reshape(planes, 8, 3, ids.shape[1])
    group_ids = (d[:, :, 0] * 65536 + d[:, :, 1] * 256 + d[:, :, 2]).reshape(planes, group)
    matches = jax.vmap(compact)(group_ids)
    picked = jnp.dot(
        matches[0].astype(BF), embed_cot, preferred_element_type=F32
    ).astype(BF)

    def cot_for(s):
        return lax.dynamic_slice_in_dim(picked, slot_plane[s] * depth, depth, axis=1)

    received = [cot_for(0)]
    for s in (1, 2, 3):
        received.append(shift_x(cot_for(planes - s), -s))
    received = jnp.concatenate(received)
    slot_ids = jnp.sum(jnp.where(matches, group_ids[:, None, :] - base, 0), axis=-1)
    slot_ids = jnp.where(jnp.any(matches, axis=-1), slot_ids, -1).reshape(-1)
    local_columns = jnp.arange(width_dev, dtype=jnp.int32)[None, :]
    slot_hot = (local_columns == slot_ids[:, None]).astype(BF)
    embed_grad = lax.dot_general(
        received, slot_hot, (((0,), (0,)), ((), ())), preferred_element_type=F32
    ).astype(BF)

    (own_w,) = pack(head_t, offs[:1], tiles)
    valid = jnp.where(x == planes - 2, (tiles_dev - tiles - off(x)) * LANES, width)
    q = jnp.stack([y, valid, off(x) * LANES, base, z, c]).astype(jnp.int32)
    ht = transposed(q, left, left_oth, depth, 256)
    left, ht = lax.optimization_barrier((left, ht))
    acc = partial_logits(
        first_kernel, [(left, left_oth, 0), (left, left_oth, 1)], [own_w, w_prev], None, 256
    )
    acc = partial_logits(mid_kernel, [(right, right_oth, 0)], [w_next], acc, 256)
    *expo, stats = logits_last(q, right, right_oth, w_across, acc, 256, chunks)

    es = []
    for e in expo:
        prev = shift_x(e, 1)
        next_ = shift_x(e, -1)
        es.append((e, next_, prev))

    st = stats[:, :3].T.reshape(3, tokens // LANES, LANES)
    both = jnp.broadcast_to(st, (lax.axis_size("vocab"), *st.shape))
    both = lax.all_to_all(both, "vocab", split_axis=0, concat_axis=0, tiled=True)

    def joined(tops, sums, hits):
        top = jnp.max(tops, axis=0)
        return top, jnp.sum(sums * jnp.exp(tops - top), axis=0), jnp.sum(hits, axis=0)

    plane_stats = jnp.stack([*joined(both[:, 0], both[:, 1], both[:, 2]), st[0]])
    parts = jnp.stack(everywhere(plane_stats))
    row_max, row_sum, hit = joined(parts[:, 0], parts[:, 1], parts[:, 2])
    scale = jnp.exp(parts[:, 3] - row_max) / row_sum
    at_target = jnp.exp(hit - row_max) / row_sum - 1.0
    coef = jnp.concatenate([scale, at_target[None]]).reshape(5, tokens).T
    coef = jnp.pad(coef, ((0, 0), (0, LANES - 5)))

    offs_y = jnp.concatenate([offs, jnp.stack([y, z, c]).astype(jnp.int32)])
    grads, pieces = [], []
    mine = None
    for i in range(chunks):
        e, next_, prev = es[i]
        half = rows // 2
        top = shift_x(prev[:half], 1)
        low = shift_x(next_[half:], -1)
        if mine is not None:
            coef, mine = lax.optimization_barrier((coef, mine))
            pieces.append(scatter_tokens(mine))
        g, keep, send = grads_of(offs_y, (e, next_, top, low, prev), coef, stats, head_t, i, 256)
        grads.append(g)
        mine = over_cores(keep, send)
    pieces.append(scatter_tokens(mine))
    hidden_grad = jnp.concatenate(pieces).astype(BF)
    head_grad = head_grad_of(ht, grads, 512)
    return (head_grad, embed_grad, hidden_grad)


def solution(mesh):
    placed = (P("dp", None), P("dp", "vocab"), P("dp"), P("dp"), P("dp", None))
    return jax.shard_map(
        step,
        mesh=mesh,
        in_specs=placed,
        out_specs=(P("dp", "vocab"), P("dp", "vocab"), P("vocab", "dp")),
        check_vma=False,
    )
```

profile of v0, /device:TPU:0, one launch (start us, length us, event | category | flops | bytes accessed | tf_op | source)
XLA Modules:
  0.0 349.3 jit_solution(3037417148325913183)
XLA Ops:
  4.4 2.9 collective-permute-start
  10.9 2.8 collective-permute-done.1.p2
  15.1 3.1 collective-permute-start.3
  20.5 4.0 %collective-permute-start.10 = (bf16[32,2688]{1,0:T(8,128)(2,1)S(1)}, bf16[32,2688]{1,0:T(8,128)(2,1)S(1)}, u32[]{:S(2)}, u32[]{:S(2)}) collective-permute-start(bf16[32,2688]{1,0:T(8,128)(2,1)S(1)} %bitcast.190), channel_id=1, source_target_pairs={{0,6},{1,7},{2,0},{3,1},{4,2},{5,3},{6,4},{7,5},{8,14},{9,15},{10,... | collective-permute-start | bytes 516104 | tf_op jit(solution)/shard_map/ppermute | solution.py:28
  24.7 1.9 collective-permute-start.12
  28.4 4.0 %collective-permute-start.7 = (bf16[128,2560]{1,0:T(8,128)(2,1)S(1)}, bf16[128,2560]{1,0:T(8,128)(2,1)S(1)}, u32[]{:S(2)}, u32[]{:S(2)}) collective-permute-start(bf16[128,2560]{1,0:T(8,128)(2,1)S(1)} %pad_maximum_fusion.2), channel_id=1, source_target_pairs={{0,4},{1,5},{2,6},{3,7},{4,0},{5,1},{6,2},{7,3},{8,12},{9,13},{10,... | collective-permute-start | bytes 1966088 | tf_op jit(solution)/shard_map/ppermute | solution.py:28
  33.4 2.2 collective-permute-start.6
  35.7 14.7 %collective-permute-start.13 = (bf16[128,2688]{1,0:T(8,128)(2,1)S(1)}, bf16[128,2688]{1,0:T(8,128)(2,1)S(1)}, u32[]{:S(2)}, u32[]{:S(2)}) collective-permute-start(bf16[128,2688]{1,0:T(8,128)(2,1)S(1)} %pad_maximum_fusion.1), channel_id=1, source_target_pairs={{0,24},{1,25},{2,26},{3,27},{4,28},{5,29},{6,30},{7,31},{8,0},{9,1... | collective-permute-start | bytes 2064392 | tf_op jit(solution)/shard_map/ppermute | solution.py:28
  50.4 2.0 collective-permute-start.14
  54.4 8.0 %collective-permute-done.8 = bf16[128,2560]{1,0:T(8,128)(2,1)S(1)} collective-permute-done((bf16[128,2560]{1,0:T(8,128)(2,1)S(1)}, bf16[128,2560]{1,0:T(8,128)(2,1)S(1)}, u32[]{:S(2)}, u32[]{:S(2)}) %collective-permute-start.8) | collective-permute-done | bytes 655392 | tf_op jit(solution)/shard_map/ppermute | solution.py:28
  64.3 2.3 collective-permute-done.13
  67.5 2.8 collective-permute-done.14
  71.1 9.7 %collective-permute-done.15 = bf16[128,2688]{1,0:T(8,128)(2,1)S(1)} collective-permute-done((bf16[128,2688]{1,0:T(8,128)(2,1)S(1)}, bf16[128,2688]{1,0:T(8,128)(2,1)S(1)}, u32[]{:S(2)}, u32[]{:S(2)}) %collective-permute-start.15) | collective-permute-done | bytes 688160 | tf_op jit(solution)/shard_map/ppermute | solution.py:28
  81.7 2.8 copy-done.1
  84.5 2.6 pack.7
  87.1 2.8 copy-done.2
  89.9 2.5 pack.5
  92.4 3.2 collective-permute-start.18
  95.6 2.8 copy-done.3
  98.4 2.5 pack.4
  100.9 2.8 copy-done.4
  106.4 4.3 %transposed.1.ht = bf16[1280,1024]{1,0:T(8,128)(2,1)S(1)} custom-call(s32[6]{0:T(128)S(1)} %stack.108.q, bf16[512,2560]{1,0:T(8,128)(2,1)} %bitcast.12.own.own1.own2, bf16[512,2560]{1,0:T(8,128)(2,1)} %collective-permute-done.9.oth.oth1.oth2), custom_call_target="tpu_custom_call" | custom-call | flops 4000000 | bytes 5000000 | tf_op jit(solution)/shard_map/transposed/pallas_call | solution.py:250
  112.3 49.6 %collective-permute-done.19.w2 = bf16[1280,640]{1,0:T(8,128)(2,1)} collective-permute-done((bf16[1280,640]{1,0:T(8,128)(2,1)}, bf16[1280,640]{1,0:T(8,128)(2,1)}, u32[]{:S(2)}, u32[]{:S(2)}) %collective-permute-start.19) | collective-permute-done | bytes 1638432 | tf_op jit(solution)/shard_map/ppermute | solution.py:16
  161.9 7.1 %shard_map.76.acc = f32[1024,640]{1,0:T(8,128)S(1)} custom-call(bf16[512,2560]{1,0:T(8,128)(2,1)} %bitcast.12.own.own1.own2, bf16[512,2560]{1,0:T(8,128)(2,1)} %collective-permute-done.9.oth.oth1.oth2, bf16[512,2560]{1,0:T(8,128)(2,1)} %bitcast.12.own.own1.own2, bf16[512,2560]{1,0:T(8,128)(2,1)} %collective-permute-done.9.oth.oth1.oth2, ...), custom_call_target="tpu_custom_call" | custom-call | flops 3355443200 | bytes 12000000 | tf_op jit(solution)/shard_map/pallas_call | solution.py:135
  169.1 5.4 %shard_map.77.acc = f32[1024,640]{1,0:T(8,128)S(1)} custom-call(bf16[512,2688]{1,0:T(8,128)(2,1)} %constant_dynamic-update-slice_fusion.own.dig_own, bf16[512,2688]{1,0:T(8,128)(2,1)} %collective-permute-done.16.oth.dig_oth, bf16[1280,640]{1,0:T(8,128)(2,1)} %collective-permute-done.18.w, f32[1024,640]{1,0:T(8,128)S(1)} %shard_map.76.acc), custom_call_target="tpu_custom_call" | custom-call | flops 1677721600 | bytes 6000000 | tf_op jit(solution)/shard_map/pallas_call | solution.py:135
  174.5 9.8 %logits_last.1 = (bf16[512,640]{1,0:T(8,128)(2,1)S(1)}, bf16[512,640]{1,0:T(8,128)(2,1)}, f32[1024,128]{1,0:T(8,128)S(1)}) custom-call(s32[6]{0:T(128)S(1)} %stack.108.q, bf16[512,2688]{1,0:T(8,128)(2,1)} %constant_dynamic-update-slice_fusion.own.dig_own, bf16[512,2688]{1,0:T(8,128)(2,1)} %collective-permute-done.16.oth.dig_oth, ...), custom_call_target="tpu_custom_call" | custom-call | flops 3355443200 | bytes 14000000 | tf_op jit(solution)/shard_map/logits_last/pallas_call | solution.py:213
  188.2 5.0 %all-to-all-start = ((f32[32,3,8,128]{3,2,1,0:T(8,128)}), f32[32,3,8,128]{3,2,1,0:T(8,128)}, u32[]{:S(2)}, u32[]{:S(2)}) async-start(f32[32,3,8,128]{3,2,1,0:T(8,128)} %broadcast_in_dim.21), calls=%async_computation | async-start | bytes 786432 | tf_op jit(solution)/shard_map/all_to_all | solution.py:492
  196.3 6.8 %all-to-all-done = f32[32,3,8,128]{3,2,1,0:T(8,128)} async-done(((f32[32,3,8,128]{3,2,1,0:T(8,128)}), f32[32,3,8,128]{3,2,1,0:T(8,128)}, u32[]{:S(2)}, u32[]{:S(2)}) %all-to-all-start) | async-done | bytes 393248 | tf_op jit(solution)/shard_map/all_to_all | solution.py:492
  208.3 2.5 collective-permute-start.21
  213.0 14.4 %collective-permute-done.21.prev = bf16[512,640]{1,0:T(8,128)(2,1)S(1)} collective-permute-done((bf16[512,640]{1,0:T(8,128)(2,1)}, bf16[512,640]{1,0:T(8,128)(2,1)S(1)}, u32[]{:S(2)}, u32[]{:S(2)}) %collective-permute-start.21) | collective-permute-done | bytes 655392 | tf_op jit(solution)/shard_map/ppermute | solution.py:16
  231.9 1.9 collective-permute-start.23
  235.9 11.9 %collective-permute-done.22.top = bf16[256,640]{1,0:T(8,128)(2,1)} collective-permute-done((bf16[256,640]{1,0:T(8,128)(2,1)}, bf16[256,640]{1,0:T(8,128)(2,1)}, u32[]{:S(2)}, u32[]{:S(2)}) %collective-permute-start.22) | collective-permute-done | bytes 327712 | tf_op jit(solution)/shard_map/ppermute | solution.py:16
  247.8 2.8 copy-done.5
  253.9 8.4 %grads.2 = (bf16[512,2432]{1,0:T(8,128)(2,1)S(1)}, f32[256,1280]{1,0:T(8,128)S(1)}, f32[256,1280]{1,0:T(8,128)}) custom-call(s32[7]{0:T(128)S(1)} %concatenate.36.offs, bf16[512,640]{1,0:T(8,128)(2,1)S(1)} %copy-done.19, bf16[512,640]{1,0:T(8,128)(2,1)S(1)} %copy-done.17, bf16[256,640]{1,0:T(8,128)(2,1)} %collective-permute-done.22.top, ...), custom_call_target="tpu_custom_call" | custom-call | flops 3187671040 | bytes 15000000 | tf_op jit(solution)/shard_map/grads/pallas_call | solution.py:305
  271.2 11.7 %collective-permute-done.27.nxt = bf16[512,640]{1,0:T(8,128)(2,1)} collective-permute-done((bf16[512,640]{1,0:T(8,128)(2,1)}, bf16[512,640]{1,0:T(8,128)(2,1)}, u32[]{:S(2)}, u32[]{:S(2)}) %collective-permute-start.27) | collective-permute-done | bytes 655392 | tf_op jit(solution)/shard_map/ppermute | solution.py:16
  284.7 2.5 collective-permute-start.30
  287.3 4.5 %convolution_convert_fusion = bf16[1280,2432]{1,0:T(8,128)(2,1)} fusion(s32[64]{0:T(128)S(1)} %select_n.148, bf16[16,1280]{1,0:T(8,128)(2,1)S(1)} %collective-permute-done.34, bf16[16,1280]{1,0:T(8,128)(2,1)S(1)} %collective-permute-done.33, bf16[16,1280]{1,0:T(8,128)(2,1)S(1)} %collective-permute-done.32, bf16[16,1280]{1,0:T(8,128)(2,1)S(1)} %get-tuple-element.52), kind=kOutput, calls=%fused_computation | convolution fusion | flops 402382848 | bytes 6390016 | tf_op jit(solution)/shard_map/dot_general | solution.py:469
  293.5 8.5 %grads.3 = (bf16[512,2432]{1,0:T(8,128)(2,1)S(1)}, f32[256,1280]{1,0:T(8,128)S(1)}, f32[256,1280]{1,0:T(8,128)S(1)}) custom-call(s32[7]{0:T(128)S(1)} %concatenate.36.offs, bf16[512,640]{1,0:T(8,128)(2,1)} %get-tuple-element.25.own, bf16[512,640]{1,0:T(8,128)(2,1)} %collective-permute-done.27.nxt, bf16[256,640]{1,0:T(8,128)(2,1)S(1)} %collective-permute-done.29.top, ...), custom_call_target="tpu_custom_call" | custom-call | flops 3187671040 | bytes 15000000 | tf_op jit(solution)/shard_map/grads/pallas_call | solution.py:305
  302.8 2.6 collective-permute-start.36
  305.7 9.2 %head_grad.1 = bf16[1280,2432]{1,0:T(8,128)(2,1)} custom-call(bf16[1280,1024]{1,0:T(8,128)(2,1)S(1)} %copy-done.9, bf16[512,2432]{1,0:T(8,128)(2,1)S(1)} %copy-done.21, bf16[512,2432]{1,0:T(8,128)(2,1)S(1)} %get-tuple-element.29.refs_1_), custom_call_target="tpu_custom_call" | custom-call | flops 6375342080 | bytes 16000000 | tf_op jit(solution)/shard_map/head_grad/pallas_call | solution.py:343
  314.9 5.6 %collective-permute-done.35 = f32[2,4,8,1280]{3,2,1,0:T(8,128)S(1)} collective-permute-done((f32[2,4,8,1280]{3,2,1,0:T(8,128)S(1)}, f32[2,4,8,1280]{3,2,1,0:T(8,128)S(1)}, u32[]{:S(2)}, u32[]{:S(2)}) %collective-permute-start.35) | collective-permute-done | bytes 327712 | tf_op jit(solution)/shard_map/ppermute | solution.py:28
  321.8 2.4 collective-permute-start.43
  325.8 2.9 collective-permute-start.39
  328.7 3.4 collective-permute-done.42
  332.3 5.4 %collective-permute-done.43 = f32[2,4,8,1280]{3,2,1,0:T(8,128)S(1)} collective-permute-done((f32[2,4,8,1280]{3,2,1,0:T(8,128)S(1)}, f32[2,4,8,1280]{3,2,1,0:T(8,128)S(1)}, u32[]{:S(2)}, u32[]{:S(2)}) %collective-permute-start.43) | collective-permute-done | bytes 327712 | tf_op jit(solution)/shard_map/ppermute | solution.py:28
  339.8 2.9 collective-permute-start.46
  342.8 3.2 collective-permute-done.45
  346.0 2.7 collective-permute-done.47
  (194 shorter events, 68.5 us)
Async XLA Ops:
  4.4 6.5 %collective-permute-start = (bf16[8,5248]{1,0:T(8,128)(2,1)S(1)}, bf16[8,5248]{1,0:T(8,128)(2,1)S(1)}, u32[]{:S(2)}, u32[]{:S(2)}) collective-permute-start(bf16[8,5248]{1,0:T(8,128)(2,1)S(1)} %concatenate.34.p0), channel_id=1, source_target_pairs={{0,96},{32,0},{64,32},{96,64},{1,97},{33,1},{65,33},{97,65},{2,98}... | collective-permute-start | bytes 251912 | tf_op jit(solution)/shard_map/ppermute | solution.py:16
  7.3 6.4 %collective-permute-start.1 = (bf16[8,5248]{1,0:T(8,128)(2,1)S(1)}, bf16[8,5248]{1,0:T(8,128)(2,1)S(1)}, u32[]{:S(2)}, u32[]{:S(2)}) collective-permute-start(bf16[8,5248]{1,0:T(8,128)(2,1)S(1)} %concatenate.34.p0), channel_id=1, source_target_pairs={{0,64},{32,96},{64,0},{96,32},{1,65},{33,97},{65,1},{97,33},{2,66}... | collective-permute-start | bytes 251912 | tf_op jit(solution)/shard_map/ppermute | solution.py:16
  8.1 6.5 %collective-permute-start.2 = (bf16[8,5248]{1,0:T(8,128)(2,1)S(1)}, bf16[8,5248]{1,0:T(8,128)(2,1)S(1)}, u32[]{:S(2)}, u32[]{:S(2)}) collective-permute-start(bf16[8,5248]{1,0:T(8,128)(2,1)S(1)} %concatenate.34.p0), channel_id=1, source_target_pairs={{0,32},{32,64},{64,96},{96,0},{1,33},{33,65},{65,97},{97,1},{2,34}... | collective-permute-start | bytes 251912 | tf_op jit(solution)/shard_map/ppermute | solution.py:16
  15.1 9.6 %collective-permute-start.3 = (bf16[32,2560]{1,0:T(8,128)(2,1)S(1)}, bf16[32,2560]{1,0:T(8,128)(2,1)S(1)}, u32[]{:S(2)}, u32[]{:S(2)}) collective-permute-start(bf16[32,2560]{1,0:T(8,128)(2,1)S(1)} %bitcast.194), channel_id=1, source_target_pairs={{0,24},{1,25},{2,26},{3,27},{4,28},{5,29},{6,30},{7,31},{8,0},{9,1... | collective-permute-start | bytes 491528 | tf_op jit(solution)/shard_map/ppermute | solution.py:28
  18.2 8.5 %collective-permute-start.4 = (bf16[32,2560]{1,0:T(8,128)(2,1)S(1)}, bf16[32,2560]{1,0:T(8,128)(2,1)S(1)}, u32[]{:S(2)}, u32[]{:S(2)}) collective-permute-start(bf16[32,2560]{1,0:T(8,128)(2,1)S(1)} %bitcast.195), channel_id=1, source_target_pairs={{0,16},{1,17},{2,18},{3,19},{4,20},{5,21},{6,22},{7,23},{8,24},{9,... | collective-permute-start | bytes 491528 | tf_op jit(solution)/shard_map/ppermute | solution.py:28
  18.8 9.6 %collective-permute-start.5 = (bf16[32,2560]{1,0:T(8,128)(2,1)S(1)}, bf16[32,2560]{1,0:T(8,128)(2,1)S(1)}, u32[]{:S(2)}, u32[]{:S(2)}) collective-permute-start(bf16[32,2560]{1,0:T(8,128)(2,1)S(1)} %bitcast.196), channel_id=1, source_target_pairs={{0,8},{1,9},{2,10},{3,11},{4,12},{5,13},{6,14},{7,15},{8,16},{9,17... | collective-permute-start | bytes 491528 | tf_op jit(solution)/shard_map/ppermute | solution.py:28
  20.5 12.9 %collective-permute-start.10 = (bf16[32,2688]{1,0:T(8,128)(2,1)S(1)}, bf16[32,2688]{1,0:T(8,128)(2,1)S(1)}, u32[]{:S(2)}, u32[]{:S(2)}) collective-permute-start(bf16[32,2688]{1,0:T(8,128)(2,1)S(1)} %bitcast.190), channel_id=1, source_target_pairs={{0,6},{1,7},{2,0},{3,1},{4,2},{5,3},{6,4},{7,5},{8,14},{9,15},{10,... | collective-permute-start | bytes 516104 | tf_op jit(solution)/shard_map/ppermute | solution.py:28
  24.5 11.1 %collective-permute-start.11 = (bf16[32,2688]{1,0:T(8,128)(2,1)S(1)}, bf16[32,2688]{1,0:T(8,128)(2,1)S(1)}, u32[]{:S(2)}, u32[]{:S(2)}) collective-permute-start(bf16[32,2688]{1,0:T(8,128)(2,1)S(1)} %bitcast.191), channel_id=1, source_target_pairs={{0,4},{1,5},{2,6},{3,7},{4,0},{5,1},{6,2},{7,3},{8,12},{9,13},{10,... | collective-permute-start | bytes 516104 | tf_op jit(solution)/shard_map/ppermute | solution.py:28
  24.7 11.0 %collective-permute-start.12 = (bf16[32,2688]{1,0:T(8,128)(2,1)S(1)}, bf16[32,2688]{1,0:T(8,128)(2,1)S(1)}, u32[]{:S(2)}, u32[]{:S(2)}) collective-permute-start(bf16[32,2688]{1,0:T(8,128)(2,1)S(1)} %bitcast.192), channel_id=1, source_target_pairs={{0,2},{1,3},{2,4},{3,5},{4,6},{5,7},{6,0},{7,1},{8,10},{9,11},{10,... | collective-permute-start | bytes 516104 | tf_op jit(solution)/shard_map/ppermute | solution.py:28
  28.4 25.9 %collective-permute-start.7 = (bf16[128,2560]{1,0:T(8,128)(2,1)S(1)}, bf16[128,2560]{1,0:T(8,128)(2,1)S(1)}, u32[]{:S(2)}, u32[]{:S(2)}) collective-permute-start(bf16[128,2560]{1,0:T(8,128)(2,1)S(1)} %pad_maximum_fusion.2), channel_id=1, source_target_pairs={{0,4},{1,5},{2,6},{3,7},{4,0},{5,1},{6,2},{7,3},{8,12},{9,13},{10,... | collective-permute-start | bytes 1966088 | tf_op jit(solution)/shard_map/ppermute | solution.py:28
  32.4 30.0 %collective-permute-start.8 = (bf16[128,2560]{1,0:T(8,128)(2,1)S(1)}, bf16[128,2560]{1,0:T(8,128)(2,1)S(1)}, u32[]{:S(2)}, u32[]{:S(2)}) collective-permute-start(bf16[128,2560]{1,0:T(8,128)(2,1)S(1)} %pad_maximum_fusion.2), channel_id=1, source_target_pairs={{0,2},{1,3},{2,4},{3,5},{4,6},{5,7},{6,0},{7,1},{8,10},{9,11},{10,... | collective-permute-start | bytes 1966088 | tf_op jit(solution)/shard_map/ppermute | solution.py:28
  33.4 28.9 %collective-permute-start.6 = (bf16[128,2560]{1,0:T(8,128)(2,1)S(1)}, bf16[128,2560]{1,0:T(8,128)(2,1)S(1)}, u32[]{:S(2)}, u32[]{:S(2)}) collective-permute-start(bf16[128,2560]{1,0:T(8,128)(2,1)S(1)} %pad_maximum_fusion.2), channel_id=1, source_target_pairs={{0,6},{1,7},{2,0},{3,1},{4,2},{5,3},{6,4},{7,5},{8,14},{9,15},{10,... | collective-permute-start | bytes 1966088 | tf_op jit(solution)/shard_map/ppermute | solution.py:28
  35.7 30.9 %collective-permute-start.13 = (bf16[128,2688]{1,0:T(8,128)(2,1)S(1)}, bf16[128,2688]{1,0:T(8,128)(2,1)S(1)}, u32[]{:S(2)}, u32[]{:S(2)}) collective-permute-start(bf16[128,2688]{1,0:T(8,128)(2,1)S(1)} %pad_maximum_fusion.1), channel_id=1, source_target_pairs={{0,24},{1,25},{2,26},{3,27},{4,28},{5,29},{6,30},{7,31},{8,0},{9,1... | collective-permute-start | bytes 2064392 | tf_op jit(solution)/shard_map/ppermute | solution.py:28
  50.4 19.9 %collective-permute-start.14 = (bf16[128,2688]{1,0:T(8,128)(2,1)S(1)}, bf16[128,2688]{1,0:T(8,128)(2,1)S(1)}, u32[]{:S(2)}, u32[]{:S(2)}) collective-permute-start(bf16[128,2688]{1,0:T(8,128)(2,1)S(1)} %pad_maximum_fusion.1), channel_id=1, source_target_pairs={{0,16},{1,17},{2,18},{3,19},{4,20},{5,21},{6,22},{7,23},{8,24},{9,... | collective-permute-start | bytes 2064392 | tf_op jit(solution)/shard_map/ppermute | solution.py:28
  54.4 26.4 %collective-permute-start.15 = (bf16[128,2688]{1,0:T(8,128)(2,1)S(1)}, bf16[128,2688]{1,0:T(8,128)(2,1)S(1)}, u32[]{:S(2)}, u32[]{:S(2)}) collective-permute-start(bf16[128,2688]{1,0:T(8,128)(2,1)S(1)} %pad_maximum_fusion.1), channel_id=1, source_target_pairs={{0,8},{1,9},{2,10},{3,11},{4,12},{5,13},{6,14},{7,15},{8,16},{9,17... | collective-permute-start | bytes 2064392 | tf_op jit(solution)/shard_map/ppermute | solution.py:28
  64.2 42.3 %collective-permute-start.9 = (bf16[512,2560]{1,0:T(8,128)(2,1)}, bf16[512,2560]{1,0:T(8,128)(2,1)}, u32[]{:S(2)}, u32[]{:S(2)}) collective-permute-start(bf16[512,2560]{1,0:T(8,128)(2,1)} %bitcast.12.own.own1.own2), channel_id=1, source_target_pairs={{0,1},{1,0},{2,3},{3,2},{4,5},{5,4},{6,7},{7,6},{8,9},{9,8},{10,11... | collective-permute-start | bytes 7864328 | tf_op jit(solution)/shard_map/ppermute | solution.py:28
  81.7 87.4 %collective-permute-start.16 = (bf16[512,2688]{1,0:T(8,128)(2,1)}, bf16[512,2688]{1,0:T(8,128)(2,1)}, u32[]{:S(2)}, u32[]{:S(2)}) collective-permute-start(bf16[512,2688]{1,0:T(8,128)(2,1)} %constant_dynamic-update-slice_fusion.own.dig_own), channel_id=1, source_target_pairs={{0,1},{1,0},{2,3},{3,2},{4,5},{5,4},{6,7},{7,6},{8,9},{9,8},{10,11... | collective-permute-start | bytes 8257544 | tf_op jit(solution)/shard_map/ppermute | solution.py:28
  87.1 74.8 %collective-permute-start.19 = (bf16[1280,640]{1,0:T(8,128)(2,1)}, bf16[1280,640]{1,0:T(8,128)(2,1)}, u32[]{:S(2)}, u32[]{:S(2)}) collective-permute-start(bf16[1280,640]{1,0:T(8,128)(2,1)} %pack.7), channel_id=1, source_target_pairs={{0,32},{32,64},{64,96},{96,0},{1,33},{33,65},{65,97},{97,1},{2,34}... | collective-permute-start | bytes 4915208 | tf_op jit(solution)/shard_map/ppermute | solution.py:16
  92.4 76.7 %collective-permute-start.18 = (bf16[1280,640]{1,0:T(8,128)(2,1)}, bf16[1280,640]{1,0:T(8,128)(2,1)}, u32[]{:S(2)}, u32[]{:S(2)}) collective-permute-start(bf16[1280,640]{1,0:T(8,128)(2,1)} %pack.5), channel_id=1, source_target_pairs={{0,96},{32,0},{64,32},{96,64},{1,97},{33,1},{65,33},{97,65},{2,98}... | collective-permute-start | bytes 4915208 | tf_op jit(solution)/shard_map/ppermute | solution.py:16
  100.9 73.6 %collective-permute-start.17 = (bf16[1280,640]{1,0:T(8,128)(2,1)}, bf16[1280,640]{1,0:T(8,128)(2,1)}, u32[]{:S(2)}, u32[]{:S(2)}) collective-permute-start(bf16[1280,640]{1,0:T(8,128)(2,1)} %pack.4), channel_id=1, source_target_pairs={{0,64},{32,96},{64,0},{96,32},{1,65},{33,97},{65,1},{97,33},{2,66}... | collective-permute-start | bytes 4915208 | tf_op jit(solution)/shard_map/ppermute | solution.py:16
  188.2 15.0 %all-to-all-start = ((f32[32,3,8,128]{3,2,1,0:T(8,128)}), f32[32,3,8,128]{3,2,1,0:T(8,128)}, u32[]{:S(2)}, u32[]{:S(2)}) async-start(f32[32,3,8,128]{3,2,1,0:T(8,128)} %broadcast_in_dim.21), calls=%async_computation | async-start | bytes 786432 | tf_op jit(solution)/shard_map/all_to_all | solution.py:492
  207.2 5.7 %collective-permute-start.25 = (f32[4,8,128]{2,1,0:T(8,128)S(1)}, f32[4,8,128]{2,1,0:T(8,128)S(1)}, u32[]{:S(2)}, u32[]{:S(2)}) collective-permute-start(f32[4,8,128]{2,1,0:T(8,128)S(1)} %get-tuple-element.59), channel_id=1, source_target_pairs={{0,64},{32,96},{64,0},{96,32},{1,65},{33,97},{65,1},{97,33},{2,66}... | collective-permute-start | bytes 49160 | tf_op jit(solution)/shard_map/ppermute | solution.py:16
  207.2 5.7 %collective-permute-start.26 = (f32[4,8,128]{2,1,0:T(8,128)S(1)}, f32[4,8,128]{2,1,0:T(8,128)S(1)}, u32[]{:S(2)}, u32[]{:S(2)}) collective-permute-start(f32[4,8,128]{2,1,0:T(8,128)S(1)} %get-tuple-element.59), channel_id=1, source_target_pairs={{0,32},{32,64},{64,96},{96,0},{1,33},{33,65},{65,97},{97,1},{2,34}... | collective-permute-start | bytes 49160 | tf_op jit(solution)/shard_map/ppermute | solution.py:16
  208.3 19.0 %collective-permute-start.21 = (bf16[512,640]{1,0:T(8,128)(2,1)}, bf16[512,640]{1,0:T(8,128)(2,1)S(1)}, u32[]{:S(2)}, u32[]{:S(2)}) collective-permute-start(bf16[512,640]{1,0:T(8,128)(2,1)} %copy-done.18), channel_id=1, source_target_pairs={{0,32},{32,64},{64,96},{96,0},{1,33},{33,65},{65,97},{97,1},{2,34}... | collective-permute-start | bytes 1966088 | tf_op jit(solution)/shard_map/ppermute | solution.py:16
  210.9 19.4 %collective-permute-start.20 = (bf16[512,640]{1,0:T(8,128)(2,1)}, bf16[512,640]{1,0:T(8,128)(2,1)S(1)}, u32[]{:S(2)}, u32[]{:S(2)}) collective-permute-start(bf16[512,640]{1,0:T(8,128)(2,1)} %copy-done.18), channel_id=1, source_target_pairs={{0,96},{32,0},{64,32},{96,64},{1,97},{33,1},{65,33},{97,65},{2,98}... | collective-permute-start | bytes 1966088 | tf_op jit(solution)/shard_map/ppermute | solution.py:16
  211.6 58.3 %collective-permute-start.28 = (bf16[512,640]{1,0:T(8,128)(2,1)}, bf16[512,640]{1,0:T(8,128)(2,1)}, u32[]{:S(2)}, u32[]{:S(2)}) collective-permute-start(bf16[512,640]{1,0:T(8,128)(2,1)} %get-tuple-element.25.own), channel_id=1, source_target_pairs={{0,32},{32,64},{64,96},{96,0},{1,33},{33,65},{65,97},{97,1},{2,34}... | collective-permute-start | bytes 1966088 | tf_op jit(solution)/shard_map/ppermute | solution.py:16
  228.9 18.9 %collective-permute-start.22 = (bf16[256,640]{1,0:T(8,128)(2,1)}, bf16[256,640]{1,0:T(8,128)(2,1)}, u32[]{:S(2)}, u32[]{:S(2)}) collective-permute-start(bf16[256,640]{1,0:T(8,128)(2,1)} %slice.158), channel_id=1, source_target_pairs={{0,32},{32,64},{64,96},{96,0},{1,33},{33,65},{65,97},{97,1},{2,34}... | collective-permute-start | bytes 983048 | tf_op jit(solution)/shard_map/ppermute | solution.py:16
  231.9 16.0 %collective-permute-start.23 = (bf16[256,640]{1,0:T(8,128)(2,1)}, bf16[256,640]{1,0:T(8,128)(2,1)}, u32[]{:S(2)}, u32[]{:S(2)}) collective-permute-start(bf16[256,640]{1,0:T(8,128)(2,1)} %slice.159), channel_id=1, source_target_pairs={{0,96},{32,0},{64,32},{96,64},{1,97},{33,1},{65,33},{97,65},{2,98}... | collective-permute-start | bytes 983048 | tf_op jit(solution)/shard_map/ppermute | solution.py:16
  264.8 27.0 %collective-permute-start.31 = (f32[256,1280]{1,0:T(8,128)}, f32[256,1280]{1,0:T(8,128)}, u32[]{:S(2)}, u32[]{:S(2)}) collective-permute-start(f32[256,1280]{1,0:T(8,128)} %get-tuple-element.27), channel_id=1, source_target_pairs={{0,1},{1,0},{2,3},{3,2},{4,5},{5,4},{6,7},{7,6},{8,9},{9,8},{10,11... | collective-permute-start | bytes 3932168 | tf_op jit(solution)/shard_map/ppermute | solution.py:28
  264.9 18.0 %collective-permute-start.27 = (bf16[512,640]{1,0:T(8,128)(2,1)}, bf16[512,640]{1,0:T(8,128)(2,1)}, u32[]{:S(2)}, u32[]{:S(2)}) collective-permute-start(bf16[512,640]{1,0:T(8,128)(2,1)} %get-tuple-element.25.own), channel_id=1, source_target_pairs={{0,96},{32,0},{64,32},{96,64},{1,97},{33,1},{65,33},{97,65},{2,98}... | collective-permute-start | bytes 1966088 | tf_op jit(solution)/shard_map/ppermute | solution.py:16
  267.0 17.7 %collective-permute-start.32 = (bf16[16,1280]{1,0:T(8,128)(2,1)S(1)}, bf16[16,1280]{1,0:T(8,128)(2,1)S(1)}, u32[]{:S(2)}, u32[]{:S(2)}) collective-permute-start(bf16[16,1280]{1,0:T(8,128)(2,1)S(1)} %get-tuple-element.55), channel_id=1, source_target_pairs={{0,96},{32,0},{64,32},{96,64},{1,97},{33,1},{65,33},{97,65},{2,98}... | collective-permute-start | bytes 122888 | tf_op jit(solution)/shard_map/ppermute | solution.py:16
  268.6 18.7 %collective-permute-start.33 = (bf16[16,1280]{1,0:T(8,128)(2,1)S(1)}, bf16[16,1280]{1,0:T(8,128)(2,1)S(1)}, u32[]{:S(2)}, u32[]{:S(2)}) collective-permute-start(bf16[16,1280]{1,0:T(8,128)(2,1)S(1)} %get-tuple-element.54), channel_id=1, source_target_pairs={{0,64},{32,96},{64,0},{96,32},{1,65},{33,97},{65,1},{97,33},{2,66}... | collective-permute-start | bytes 122888 | tf_op jit(solution)/shard_map/ppermute | solution.py:16
  269.9 17.4 %collective-permute-start.34 = (bf16[16,1280]{1,0:T(8,128)(2,1)S(1)}, bf16[16,1280]{1,0:T(8,128)(2,1)S(1)}, u32[]{:S(2)}, u32[]{:S(2)}) collective-permute-start(bf16[16,1280]{1,0:T(8,128)(2,1)S(1)} %get-tuple-element.53), channel_id=1, source_target_pairs={{0,32},{32,64},{64,96},{96,0},{1,33},{33,65},{65,97},{97,1},{2,34}... | collective-permute-start | bytes 122888 | tf_op jit(solution)/shard_map/ppermute | solution.py:16
  282.9 10.5 %collective-permute-start.29 = (bf16[256,640]{1,0:T(8,128)(2,1)S(1)}, bf16[256,640]{1,0:T(8,128)(2,1)S(1)}, u32[]{:S(2)}, u32[]{:S(2)}) collective-permute-start(bf16[256,640]{1,0:T(8,128)(2,1)S(1)} %slice.168), channel_id=1, source_target_pairs={{0,32},{32,64},{64,96},{96,0},{1,33},{33,65},{65,97},{97,1},{2,34}... | collective-permute-start | bytes 983048 | tf_op jit(solution)/shard_map/ppermute | solution.py:16
  284.7 8.7 %collective-permute-start.30 = (bf16[256,640]{1,0:T(8,128)(2,1)S(1)}, bf16[256,640]{1,0:T(8,128)(2,1)S(1)}, u32[]{:S(2)}, u32[]{:S(2)}) collective-permute-start(bf16[256,640]{1,0:T(8,128)(2,1)S(1)} %slice.169), channel_id=1, source_target_pairs={{0,96},{32,0},{64,32},{96,64},{1,97},{33,1},{65,33},{97,65},{2,98}... | collective-permute-start | bytes 983048 | tf_op jit(solution)/shard_map/ppermute | solution.py:16
  302.0 18.7 %collective-permute-start.41 = (f32[256,1280]{1,0:T(8,128)S(1)}, f32[256,1280]{1,0:T(8,128)S(1)}, u32[]{:S(2)}, u32[]{:S(2)}) collective-permute-start(f32[256,1280]{1,0:T(8,128)S(1)} %get-tuple-element.32), channel_id=1, source_target_pairs={{0,1},{1,0},{2,3},{3,2},{4,5},{5,4},{6,7},{7,6},{8,9},{9,8},{10,11... | collective-permute-start | bytes 3932168 | tf_op jit(solution)/shard_map/ppermute | solution.py:28
  302.1 18.4 %collective-permute-start.35 = (f32[2,4,8,1280]{3,2,1,0:T(8,128)S(1)}, f32[2,4,8,1280]{3,2,1,0:T(8,128)S(1)}, u32[]{:S(2)}, u32[]{:S(2)}) collective-permute-start(f32[2,4,8,1280]{3,2,1,0:T(8,128)S(1)} %get-tuple-element.38), channel_id=1, source_target_pairs={{0,8},{1,9},{2,10},{3,11},{4,12},{5,13},{6,14},{7,15},{8,16},{9,17... | collective-permute-start | bytes 983048 | tf_op jit(solution)/shard_map/ppermute | solution.py:28
  302.8 17.7 %collective-permute-start.36 = (f32[2,4,8,1280]{3,2,1,0:T(8,128)S(1)}, f32[2,4,8,1280]{3,2,1,0:T(8,128)S(1)}, u32[]{:S(2)}, u32[]{:S(2)}) collective-permute-start(f32[2,4,8,1280]{3,2,1,0:T(8,128)S(1)} %get-tuple-element.40), channel_id=1, source_target_pairs={{0,24},{1,25},{2,26},{3,27},{4,28},{5,29},{6,30},{7,31},{8,0},{9,1... | collective-permute-start | bytes 983048 | tf_op jit(solution)/shard_map/ppermute | solution.py:28
  305.5 15.1 %collective-permute-start.37 = (f32[2,4,8,1280]{3,2,1,0:T(8,128)S(1)}, f32[2,4,8,1280]{3,2,1,0:T(8,128)S(1)}, u32[]{:S(2)}, u32[]{:S(2)}) collective-permute-start(f32[2,4,8,1280]{3,2,1,0:T(8,128)S(1)} %get-tuple-element.39), channel_id=1, source_target_pairs={{0,16},{1,17},{2,18},{3,19},{4,20},{5,21},{6,22},{7,23},{8,24},{9,... | collective-permute-start | bytes 983048 | tf_op jit(solution)/shard_map/ppermute | solution.py:28
  320.9 11.2 %collective-permute-start.42 = (f32[2,4,8,1280]{3,2,1,0:T(8,128)S(1)}, f32[2,4,8,1280]{3,2,1,0:T(8,128)S(1)}, u32[]{:S(2)}, u32[]{:S(2)}) collective-permute-start(f32[2,4,8,1280]{3,2,1,0:T(8,128)S(1)} %get-tuple-element.41), channel_id=1, source_target_pairs={{0,8},{1,9},{2,10},{3,11},{4,12},{5,13},{6,14},{7,15},{8,16},{9,17... | collective-permute-start | bytes 983048 | tf_op jit(solution)/shard_map/ppermute | solution.py:28
  321.8 15.9 %collective-permute-start.43 = (f32[2,4,8,1280]{3,2,1,0:T(8,128)S(1)}, f32[2,4,8,1280]{3,2,1,0:T(8,128)S(1)}, u32[]{:S(2)}, u32[]{:S(2)}) collective-permute-start(f32[2,4,8,1280]{3,2,1,0:T(8,128)S(1)} %get-tuple-element.43), channel_id=1, source_target_pairs={{0,24},{1,25},{2,26},{3,27},{4,28},{5,29},{6,30},{7,31},{8,0},{9,1... | collective-permute-start | bytes 983048 | tf_op jit(solution)/shard_map/ppermute | solution.py:28
  324.2 15.1 %collective-permute-start.44 = (f32[2,4,8,1280]{3,2,1,0:T(8,128)S(1)}, f32[2,4,8,1280]{3,2,1,0:T(8,128)S(1)}, u32[]{:S(2)}, u32[]{:S(2)}) collective-permute-start(f32[2,4,8,1280]{3,2,1,0:T(8,128)S(1)} %get-tuple-element.42), channel_id=1, source_target_pairs={{0,16},{1,17},{2,18},{3,19},{4,20},{5,21},{6,22},{7,23},{8,24},{9,... | collective-permute-start | bytes 983048 | tf_op jit(solution)/shard_map/ppermute | solution.py:28
  325.4 17.4 %collective-permute-start.38 = (f32[2,8,1280]{2,1,0:T(8,128)S(1)}, f32[2,8,1280]{2,1,0:T(8,128)S(1)}, u32[]{:S(2)}, u32[]{:S(2)}) collective-permute-start(f32[2,8,1280]{2,1,0:T(8,128)S(1)} %get-tuple-element.46), channel_id=1, source_target_pairs={{0,2},{1,3},{2,4},{3,5},{4,6},{5,7},{6,0},{7,1},{8,10},{9,11},{10,... | collective-permute-start | bytes 245768 | tf_op jit(solution)/shard_map/ppermute | solution.py:28
  325.8 16.9 %collective-permute-start.39 = (f32[2,8,1280]{2,1,0:T(8,128)S(1)}, f32[2,8,1280]{2,1,0:T(8,128)S(1)}, u32[]{:S(2)}, u32[]{:S(2)}) collective-permute-start(f32[2,8,1280]{2,1,0:T(8,128)S(1)} %get-tuple-element.48), channel_id=1, source_target_pairs={{0,6},{1,7},{2,0},{3,1},{4,2},{5,3},{6,4},{7,5},{8,14},{9,15},{10,... | collective-permute-start | bytes 245768 | tf_op jit(solution)/shard_map/ppermute | solution.py:28
  332.1 10.6 %collective-permute-start.40 = (f32[2,8,1280]{2,1,0:T(8,128)S(1)}, f32[2,8,1280]{2,1,0:T(8,128)S(1)}, u32[]{:S(2)}, u32[]{:S(2)}) collective-permute-start(f32[2,8,1280]{2,1,0:T(8,128)S(1)} %get-tuple-element.47), channel_id=1, source_target_pairs={{0,4},{1,5},{2,6},{3,7},{4,0},{5,1},{6,2},{7,3},{8,12},{9,13},{10,... | collective-permute-start | bytes 245768 | tf_op jit(solution)/shard_map/ppermute | solution.py:28
  339.4 6.6 %collective-permute-start.45 = (f32[2,8,1280]{2,1,0:T(8,128)S(1)}, f32[2,8,1280]{2,1,0:T(8,128)S(1)}, u32[]{:S(2)}, u32[]{:S(2)}) collective-permute-start(f32[2,8,1280]{2,1,0:T(8,128)S(1)} %get-tuple-element.49), channel_id=1, source_target_pairs={{0,2},{1,3},{2,4},{3,5},{4,6},{5,7},{6,0},{7,1},{8,10},{9,11},{10,... | collective-permute-start | bytes 245768 | tf_op jit(solution)/shard_map/ppermute | solution.py:28
  339.8 6.2 %collective-permute-start.46 = (f32[2,8,1280]{2,1,0:T(8,128)S(1)}, f32[2,8,1280]{2,1,0:T(8,128)S(1)}, u32[]{:S(2)}, u32[]{:S(2)}) collective-permute-start(f32[2,8,1280]{2,1,0:T(8,128)S(1)} %get-tuple-element.51), channel_id=1, source_target_pairs={{0,6},{1,7},{2,0},{3,1},{4,2},{5,3},{6,4},{7,5},{8,14},{9,15},{10,... | collective-permute-start | bytes 245768 | tf_op jit(solution)/shard_map/ppermute | solution.py:28
  342.7 5.9 %collective-permute-start.47 = (f32[2,8,1280]{2,1,0:T(8,128)S(1)}, f32[2,8,1280]{2,1,0:T(8,128)S(1)}, u32[]{:S(2)}, u32[]{:S(2)}) collective-permute-start(f32[2,8,1280]{2,1,0:T(8,128)S(1)} %get-tuple-element.50), channel_id=1, source_target_pairs={{0,4},{1,5},{2,6},{3,7},{4,0},{5,1},{6,2},{7,3},{8,12},{9,13},{10,... | collective-permute-start | bytes 245768 | tf_op jit(solution)/shard_map/ppermute | solution.py:28
  (25 other events, 421.0 us)
where the time goes:
time: 351 us; the launch traced here: 349 us
  waiting for transfers between devices  147 us (42%)
  starting transfers between devices  80.1 us (23%)
  Pallas kernels  61.8 us (18%)
  local copies, waits for them, and re-layouts  43.8 us (12%)
  other arithmetic  11 us (3%)
  matrix products  4.98 us (1%)
    ppermute x20, waiting for transfers between devices, shift_x(): return lax.ppermute(a, 'dp', [(i, (i + s) % n) for i in range(n)])  93.1 us
    ppermute x28, starting transfers between devices, shift_v(): return lax.ppermute(a, 'vocab', vocab_perm(dy, dz, dc))  49.6 us
    ppermute x28, waiting for transfers between devices, shift_v(): return lax.ppermute(a, 'vocab', vocab_perm(dy, dz, dc))  46.6 us
    unnamed x55, local copies, waits for them, and re-layouts  29.3 us
    ppermute x20, starting transfers between devices, shift_x(): return lax.ppermute(a, 'dp', [(i, (i + s) % n) for i in range(n)])  25.5 us
    pallas_call x2, Pallas kernels, grads_of(): pl.pallas_call(grad_kernel, grid_spec=pltpu.PrefetchScalarGridSpec(num_sc...  16.9 us
    pallas_call x2, Pallas kernels, partial_logits(): pl.pallas_call(kernel, grid=(steps,), in_specs=specs, out_specs=whole, ou...  12.5 us
    pallas_call x1, Pallas kernels, logits_last(): pl.pallas_call(last_kernel, grid_spec=pltpu.PrefetchScalarGridSpec(num_sc...  9.81 us
  transfers between devices with their start and end apart: 49, of which 21 were waited for; matrix products, arithmetic and copies ran while one was open for 7% of the time, Pallas kernels for 12%

commit v1 on v0

--- a/solution.py
+++ b/solution.py
@@ -7,6 +7,7 @@
 
 
 LANES = 128
+STEP = 640
 BF = jnp.bfloat16
 F32 = jnp.float32
 
@@ -32,30 +33,28 @@
     return pltpu.CompilerParams(vmem_limit_bytes=mib * 2**20)
 
 
-def pack_kernel(offs, *refs):
-    n = len(refs) // 2
-    for src, dst in zip(refs[:n], refs[n:]):
-        dst[...] = src[...]
+def pack_kernel(offs, src, dst, sem):
+    start = pl.multiple_of(offs[0] * LANES, LANES)
+    copy = pltpu.make_async_copy(src.at[:, pl.ds(start, dst.shape[1])], dst, sem)
+    copy.start()
+    copy.wait()
 
 
 def pack(head_t, offs, tiles):
-    rows, n = head_t.shape[0], offs.shape[0]
-
-    def at(s):
-        return lambda t, o: (0, o[s] + t)
-
+    shape = (head_t.shape[0], tiles * LANES)
     return pl.pallas_call(
         pack_kernel,
         grid_spec=pltpu.PrefetchScalarGridSpec(
             num_scalar_prefetch=1,
-            grid=(tiles,),
-            in_specs=[pl.BlockSpec((rows, LANES), at(s)) for s in range(n)],
-            out_specs=[pl.BlockSpec((rows, LANES), lambda t, o: (0, t))] * n,
-        ),
-        out_shape=[jax.ShapeDtypeStruct((rows, tiles * LANES), BF)] * n,
-        compiler_params=vmem(6),
+            grid=(1,),
+            in_specs=[pl.BlockSpec(memory_space=pltpu.HBM)],
+            out_specs=pl.BlockSpec(shape, lambda i, o: (0, 0)),
+            scratch_shapes=[pltpu.SemaphoreType.DMA],
+        ),
+        out_shape=jax.ShapeDtypeStruct(shape, BF),
+        compiler_params=vmem(60),
         name="pack",
-    )(offs, *([head_t] * n))
+    )(offs, head_t)
 
 
 def assemble_kernel(at, p0, p1, p2, p3, left, right):
@@ -413,7 +412,7 @@
     ids = token_ids.reshape(8, group // 8)
 
     def base_256(a):
-        return [a // 65536, (a // 256) % 256, a % 256]
+        return [a >> 16, (a >> 8) & 255, a & 255]
 
     digits = jnp.concatenate(
         [*base_256(tgt), jnp.zeros((8, LANES - 3 - 3 * ids.shape[1]), jnp.int32), *base_256(ids)],
@@ -423,7 +422,7 @@
     row_parts = everywhere(jnp.concatenate([rows_mine, digits], axis=1))
     moved = {}
     for s in (1, 3, 2):
-        (block,) = pack(head_t, offs[s : s + 1], tiles)
+        block = pack(head_t, offs[s : s + 1], tiles)
         moved[s] = shift_x(block, s)
     w_prev, w_across, w_next = moved[1], moved[2], moved[3]
 
@@ -470,16 +469,15 @@
         received, slot_hot, (((0,), (0,)), ((), ())), preferred_element_type=F32
     ).astype(BF)
 
-    (own_w,) = pack(head_t, offs[:1], tiles)
+    own_w = pack(head_t, offs[:1], tiles)
     valid = jnp.where(x == planes - 2, (tiles_dev - tiles - off(x)) * LANES, width)
     q = jnp.stack([y, valid, off(x) * LANES, base, z, c]).astype(jnp.int32)
     ht = transposed(q, left, left_oth, depth, 256)
-    left, ht = lax.optimization_barrier((left, ht))
     acc = partial_logits(
-        first_kernel, [(left, left_oth, 0), (left, left_oth, 1)], [own_w, w_prev], None, 256
+        first_kernel, [(left, left_oth, 0), (left, left_oth, 1)], [own_w, w_prev], None, STEP
     )
-    acc = partial_logits(mid_kernel, [(right, right_oth, 0)], [w_next], acc, 256)
-    *expo, stats = logits_last(q, right, right_oth, w_across, acc, 256, chunks)
+    acc = partial_logits(mid_kernel, [(right, right_oth, 0)], [w_next], acc, STEP)
+    *expo, stats = logits_last(q, right, right_oth, w_across, acc, depth, chunks)
 
     es = []
     for e in expo:

time: 351 us -> 340 us (0.969)
  local copies, waits for them, and re-layouts: 43.8 us -> 31 us
  waiting for transfers between devices: 147 us -> 153 us
    ppermute x28, starting transfers between devices: 49.6 us -> 36.7 us  [shift_v(): return lax.ppermute(a, 'vocab', vocab_perm(dy, dz, dc))]
    unnamed x55 -> x41, local copies, waits for them, and re-layouts: 29.3 us -> 17.1 us
    all_to_all x1, starting transfers between devices: 5.03 us -> 13.3 us  [step(): lax.all_to_all(both, 'vocab', split_axis=0, concat_axis=0, tiled=True)]
  transfers between devices with their start and end apart: 49 -> 49, of which waited for: 21 -> 20; matrix products, arithmetic and copies ran while one was open for 7% -> 7% of each run, Pallas kernels for 12% -> 13%
where the time goes in v1:
time: 340 us; the launch traced here: 339 us
  waiting for transfers between devices  153 us (45%)
  starting transfers between devices  77.7 us (23%)
  Pallas kernels  59.9 us (18%)
  local copies, waits for them, and re-layouts  31 us (9%)
  other arithmetic  11 us (3%)
  matrix products  4.98 us (1%)
    ppermute x20, waiting for transfers between devices, shift_x(): return lax.ppermute(a, 'dp', [(i, (i + s) % n) for i in range(n)])  96.2 us
    ppermute x28, waiting for transfers between devices, shift_v(): return lax.ppermute(a, 'vocab', vocab_perm(dy, dz, dc))  49.9 us
    ppermute x28, starting transfers between devices, shift_v(): return lax.ppermute(a, 'vocab', vocab_perm(dy, dz, dc))  36.7 us
    ppermute x20, starting transfers between devices, shift_x(): return lax.ppermute(a, 'dp', [(i, (i + s) % n) for i in range(n)])  27.6 us
    unnamed x41, local copies, waits for them, and re-layouts  17.1 us
    pallas_call x2, Pallas kernels, grads_of(): pl.pallas_call(grad_kernel, grid_spec=pltpu.PrefetchScalarGridSpec(num_sc...  16.7 us
    all_to_all x1, starting transfers between devices, step(): lax.all_to_all(both, 'vocab', split_axis=0, concat_axis=0, tiled=True)  13.3 us
    pallas_call x2, Pallas kernels, partial_logits(): pl.pallas_call(kernel, grid=(steps,), in_specs=specs, out_specs=whole, ou...  11.6 us
  transfers between devices with their start and end apart: 49, of which 20 were waited for; matrix products, arithmetic and copies ran while one was open for 7% of the time, Pallas kernels for 13%

profile of v1, /device:TPU:0, one launch (start us, length us, event | category | flops | bytes accessed | tf_op | source)
XLA Modules:
  0.0 338.6 jit_solution(8715341572732982658)
XLA Ops:
  3.8 1.6 collective-permute-start.2
  5.4 2.7 collective-permute-start.1
  9.7 2.5 collective-permute-done.1.p2
  13.2 1.6 collective-permute-start.5
  14.8 2.9 collective-permute-start.4
  19.1 1.9 collective-permute-start.12
  21.0 3.6 %collective-permute-start.11 = (bf16[32,2688]{1,0:T(8,128)(2,1)S(1)}, bf16[32,2688]{1,0:T(8,128)(2,1)S(1)}, u32[]{:S(2)}, u32[]{:S(2)}) collective-permute-start(bf16[32,2688]{1,0:T(8,128)(2,1)S(1)} %bitcast.191), channel_id=1, source_target_pairs={{0,4},{1,5},{2,6},{3,7},{4,0},{5,1},{6,2},{7,3},{8,12},{9,13},{10,... | collective-permute-start | bytes 516104 | tf_op jit(solution)/shard_map/ppermute | solution.py:29
  27.4 2.4 collective-permute-start.7
  30.8 2.3 collective-permute-done.11
  33.1 10.9 %collective-permute-done.10 = bf16[32,2688]{1,0:T(8,128)(2,1)S(1)} collective-permute-done((bf16[32,2688]{1,0:T(8,128)(2,1)S(1)}, bf16[32,2688]{1,0:T(8,128)(2,1)S(1)}, u32[]{:S(2)}, u32[]{:S(2)}) %collective-permute-start.10) | collective-permute-done | bytes 172064 | tf_op jit(solution)/shard_map/ppermute | solution.py:29
  44.1 3.2 collective-permute-start.13
  50.3 8.4 %collective-permute-done.7 = bf16[128,2560]{1,0:T(8,128)(2,1)S(1)} collective-permute-done((bf16[128,2560]{1,0:T(8,128)(2,1)S(1)}, bf16[128,2560]{1,0:T(8,128)(2,1)S(1)}, u32[]{:S(2)}, u32[]{:S(2)}) %collective-permute-start.7) | collective-permute-done | bytes 655392 | tf_op jit(solution)/shard_map/ppermute | solution.py:29
  58.9 1.8 pad_maximum_fusion
  60.8 7.6 %collective-permute-done.13 = bf16[128,2688]{1,0:T(8,128)(2,1)S(1)} collective-permute-done((bf16[128,2688]{1,0:T(8,128)(2,1)S(1)}, bf16[128,2688]{1,0:T(8,128)(2,1)S(1)}, u32[]{:S(2)}, u32[]{:S(2)}) %collective-permute-start.13) | collective-permute-done | bytes 688160 | tf_op jit(solution)/shard_map/ppermute | solution.py:29
  71.1 2.6 pack.7
  74.8 2.6 pack.5
  77.4 2.3 collective-permute-start.18
  79.7 2.6 pack.4
  83.8 2.6 pack.6.w1
  87.1 26.5 %collective-permute-done.19.w2 = bf16[1280,640]{1,0:T(8,128)(2,1)} collective-permute-done((bf16[1280,640]{1,0:T(8,128)(2,1)}, bf16[1280,640]{1,0:T(8,128)(2,1)}, u32[]{:S(2)}, u32[]{:S(2)}) %collective-permute-start.19) | collective-permute-done | bytes 1638432 | tf_op jit(solution)/shard_map/ppermute | solution.py:17
  115.0 7.2 %shard_map.76.acc = f32[1024,640]{1,0:T(8,128)S(1)} custom-call(bf16[512,2560]{1,0:T(8,128)(2,1)} %bitcast.18.own.own1.own2, bf16[512,2560]{1,0:T(8,128)(2,1)} %collective-permute-done.9.oth.oth1.oth2, bf16[512,2560]{1,0:T(8,128)(2,1)} %bitcast.18.own.own1.own2, bf16[512,2560]{1,0:T(8,128)(2,1)} %collective-permute-done.9.oth.oth1.oth2, ...), custom_call_target="tpu_custom_call" | custom-call | flops 3355443200 | bytes 12000000 | tf_op jit(solution)/shard_map/pallas_call | solution.py:134
  122.1 28.5 %collective-permute-done.18.w = bf16[1280,640]{1,0:T(8,128)(2,1)} collective-permute-done((bf16[1280,640]{1,0:T(8,128)(2,1)}, bf16[1280,640]{1,0:T(8,128)(2,1)}, u32[]{:S(2)}, u32[]{:S(2)}) %collective-permute-start.18) | collective-permute-done | bytes 1638432 | tf_op jit(solution)/shard_map/ppermute | solution.py:17
  150.6 4.4 %shard_map.77.acc = f32[1024,640]{1,0:T(8,128)S(1)} custom-call(bf16[512,2688]{1,0:T(8,128)(2,1)} %constant_dynamic-update-slice_fusion.own.dig_own, bf16[512,2688]{1,0:T(8,128)(2,1)} %collective-permute-done.16.oth.dig_oth, bf16[1280,640]{1,0:T(8,128)(2,1)} %collective-permute-done.18.w, f32[1024,640]{1,0:T(8,128)S(1)} %shard_map.76.acc), custom_call_target="tpu_custom_call" | custom-call | flops 1677721600 | bytes 6000000 | tf_op jit(solution)/shard_map/pallas_call | solution.py:134
  155.1 6.9 %logits_last.1 = (bf16[512,640]{1,0:T(8,128)(2,1)S(1)}, bf16[512,640]{1,0:T(8,128)(2,1)}, f32[1024,128]{1,0:T(8,128)S(1)}) custom-call(s32[6]{0:T(128)S(1)} %stack.102.q, bf16[512,2688]{1,0:T(8,128)(2,1)} %constant_dynamic-update-slice_fusion.own.dig_own, bf16[512,2688]{1,0:T(8,128)(2,1)} %collective-permute-done.16.oth.dig_oth, ...), custom_call_target="tpu_custom_call" | custom-call | flops 3355443200 | bytes 14000000 | tf_op jit(solution)/shard_map/logits_last/pallas_call | solution.py:212
  165.8 13.3 %all-to-all-start = ((f32[32,3,8,128]{3,2,1,0:T(8,128)}), f32[32,3,8,128]{3,2,1,0:T(8,128)}, u32[]{:S(2)}, u32[]{:S(2)}) async-start(f32[32,3,8,128]{3,2,1,0:T(8,128)} %broadcast_in_dim.21), calls=%async_computation | async-start | bytes 786432 | tf_op jit(solution)/shard_map/all_to_all | solution.py:490
  182.3 6.8 %all-to-all-done = f32[32,3,8,128]{3,2,1,0:T(8,128)} async-done(((f32[32,3,8,128]{3,2,1,0:T(8,128)}), f32[32,3,8,128]{3,2,1,0:T(8,128)}, u32[]{:S(2)}, u32[]{:S(2)}) %all-to-all-start) | async-done | bytes 393248 | tf_op jit(solution)/shard_map/all_to_all | solution.py:490
  192.2 2.0 collective-permute-start.26
  195.8 1.9 collective-permute-start.20
  198.0 15.4 %collective-permute-done.21.prev = bf16[512,640]{1,0:T(8,128)(2,1)S(1)} collective-permute-done((bf16[512,640]{1,0:T(8,128)(2,1)}, bf16[512,640]{1,0:T(8,128)(2,1)S(1)}, u32[]{:S(2)}, u32[]{:S(2)}) %collective-permute-start.21) | collective-permute-done | bytes 655392 | tf_op jit(solution)/shard_map/ppermute | solution.py:17
  216.8 3.1 collective-permute-start.23
  222.0 11.6 %collective-permute-done.22.top = bf16[256,640]{1,0:T(8,128)(2,1)} collective-permute-done((bf16[256,640]{1,0:T(8,128)(2,1)}, bf16[256,640]{1,0:T(8,128)(2,1)}, u32[]{:S(2)}, u32[]{:S(2)}) %collective-permute-start.22) | collective-permute-done | bytes 327712 | tf_op jit(solution)/shard_map/ppermute | solution.py:17
  233.6 2.8 copy-done.1
  239.7 8.4 %grads.2 = (bf16[512,2432]{1,0:T(8,128)(2,1)S(1)}, f32[256,1280]{1,0:T(8,128)S(1)}, f32[256,1280]{1,0:T(8,128)}) custom-call(s32[7]{0:T(128)S(1)} %concatenate.36.offs, bf16[512,640]{1,0:T(8,128)(2,1)S(1)} %copy-done.12, bf16[512,640]{1,0:T(8,128)(2,1)S(1)} %copy-done.10, bf16[256,640]{1,0:T(8,128)(2,1)} %collective-permute-done.22.top, ...), custom_call_target="tpu_custom_call" | custom-call | flops 3187671040 | bytes 15000000 | tf_op jit(solution)/shard_map/grads/pallas_call | solution.py:304
  253.5 2.0 collective-permute-start.33
  257.7 11.1 %collective-permute-done.27.nxt = bf16[512,640]{1,0:T(8,128)(2,1)} collective-permute-done((bf16[512,640]{1,0:T(8,128)(2,1)}, bf16[512,640]{1,0:T(8,128)(2,1)}, u32[]{:S(2)}, u32[]{:S(2)}) %collective-permute-start.27) | collective-permute-done | bytes 655392 | tf_op jit(solution)/shard_map/ppermute | solution.py:17
  270.0 3.1 collective-permute-start.30
  273.1 4.5 %convolution_convert_fusion = bf16[1280,2432]{1,0:T(8,128)(2,1)} fusion(s32[64]{0:T(128)S(1)} %select_n.91, bf16[16,1280]{1,0:T(8,128)(2,1)S(1)} %collective-permute-done.34, bf16[16,1280]{1,0:T(8,128)(2,1)S(1)} %collective-permute-done.33, bf16[16,1280]{1,0:T(8,128)(2,1)S(1)} %collective-permute-done.32, bf16[16,1280]{1,0:T(8,128)(2,1)S(1)} %get-tuple-element.46), kind=kOutput, calls=%fused_computation | convolution fusion | flops 402382848 | bytes 6390016 | tf_op jit(solution)/shard_map/dot_general | solution.py:468
  277.7 4.5 %transposed.1.ht = bf16[1280,1024]{1,0:T(8,128)(2,1)S(1)} custom-call(s32[6]{0:T(128)S(1)} %stack.102.q, bf16[512,2560]{1,0:T(8,128)(2,1)} %bitcast.18.own.own1.own2, bf16[512,2560]{1,0:T(8,128)(2,1)} %collective-permute-done.9.oth.oth1.oth2), custom_call_target="tpu_custom_call" | custom-call | flops 4000000 | bytes 5000000 | tf_op jit(solution)/shard_map/transposed/pallas_call | solution.py:249
  283.8 8.3 %grads.3 = (bf16[512,2432]{1,0:T(8,128)(2,1)S(1)}, f32[256,1280]{1,0:T(8,128)S(1)}, f32[256,1280]{1,0:T(8,128)S(1)}) custom-call(s32[7]{0:T(128)S(1)} %concatenate.36.offs, bf16[512,640]{1,0:T(8,128)(2,1)} %get-tuple-element.21.own, bf16[512,640]{1,0:T(8,128)(2,1)} %collective-permute-done.27.nxt, bf16[256,640]{1,0:T(8,128)(2,1)S(1)} %collective-permute-done.29.top, ...), custom_call_target="tpu_custom_call" | custom-call | flops 3187671040 | bytes 15000000 | tf_op jit(solution)/shard_map/grads/pallas_call | solution.py:304
  292.8 2.0 collective-permute-start.37
  296.3 9.2 %head_grad.1 = bf16[1280,2432]{1,0:T(8,128)(2,1)} custom-call(bf16[1280,1024]{1,0:T(8,128)(2,1)S(1)} %transposed.1.ht, bf16[512,2432]{1,0:T(8,128)(2,1)S(1)} %copy-done.14, bf16[512,2432]{1,0:T(8,128)(2,1)S(1)} %get-tuple-element.25.refs_1_), custom_call_target="tpu_custom_call" | custom-call | flops 6375342080 | bytes 16000000 | tf_op jit(solution)/shard_map/head_grad/pallas_call | solution.py:342
  305.6 5.1 %collective-permute-done.35 = f32[2,4,8,1280]{3,2,1,0:T(8,128)S(1)} collective-permute-done((f32[2,4,8,1280]{3,2,1,0:T(8,128)S(1)}, f32[2,4,8,1280]{3,2,1,0:T(8,128)S(1)}, u32[]{:S(2)}, u32[]{:S(2)}) %collective-permute-start.35) | collective-permute-done | bytes 327712 | tf_op jit(solution)/shard_map/ppermute | solution.py:29
  312.4 3.4 collective-permute-start.44
  316.3 2.1 collective-permute-start.40
  318.5 3.7 %collective-permute-done.42 = f32[2,4,8,1280]{3,2,1,0:T(8,128)S(1)} collective-permute-done((f32[2,4,8,1280]{3,2,1,0:T(8,128)S(1)}, f32[2,4,8,1280]{3,2,1,0:T(8,128)S(1)}, u32[]{:S(2)}, u32[]{:S(2)}) %collective-permute-start.42) | collective-permute-done | bytes 327712 | tf_op jit(solution)/shard_map/ppermute | solution.py:29
  323.2 7.2 %collective-permute-done.44 = f32[2,4,8,1280]{3,2,1,0:T(8,128)S(1)} collective-permute-done((f32[2,4,8,1280]{3,2,1,0:T(8,128)S(1)}, f32[2,4,8,1280]{3,2,1,0:T(8,128)S(1)}, u32[]{:S(2)}, u32[]{:S(2)}) %collective-permute-start.44) | collective-permute-done | bytes 327712 | tf_op jit(solution)/shard_map/ppermute | solution.py:29
  331.0 2.0 collective-permute-start.47
  334.1 3.0 collective-permute-done.45
  (181 shorter events, 61.3 us)
Async XLA Ops:
  3.8 5.8 %collective-permute-start.2 = (bf16[8,5248]{1,0:T(8,128)(2,1)S(1)}, bf16[8,5248]{1,0:T(8,128)(2,1)S(1)}, u32[]{:S(2)}, u32[]{:S(2)}) collective-permute-start(bf16[8,5248]{1,0:T(8,128)(2,1)S(1)} %concatenate.34.p0), channel_id=1, source_target_pairs={{0,32},{32,64},{64,96},{96,0},{1,33},{33,65},{65,97},{97,1},{2,34}... | collective-permute-start | bytes 251912 | tf_op jit(solution)/shard_map/ppermute | solution.py:17
  5.4 6.7 %collective-permute-start.1 = (bf16[8,5248]{1,0:T(8,128)(2,1)S(1)}, bf16[8,5248]{1,0:T(8,128)(2,1)S(1)}, u32[]{:S(2)}, u32[]{:S(2)}) collective-permute-start(bf16[8,5248]{1,0:T(8,128)(2,1)S(1)} %concatenate.34.p0), channel_id=1, source_target_pairs={{0,64},{32,96},{64,0},{96,32},{1,65},{33,97},{65,1},{97,33},{2,66}... | collective-permute-start | bytes 251912 | tf_op jit(solution)/shard_map/ppermute | solution.py:17
  13.2 12.1 %collective-permute-start.5 = (bf16[32,2560]{1,0:T(8,128)(2,1)S(1)}, bf16[32,2560]{1,0:T(8,128)(2,1)S(1)}, u32[]{:S(2)}, u32[]{:S(2)}) collective-permute-start(bf16[32,2560]{1,0:T(8,128)(2,1)S(1)} %bitcast.194), channel_id=1, source_target_pairs={{0,8},{1,9},{2,10},{3,11},{4,12},{5,13},{6,14},{7,15},{8,16},{9,17... | collective-permute-start | bytes 491528 | tf_op jit(solution)/shard_map/ppermute | solution.py:29
  14.8 11.4 %collective-permute-start.4 = (bf16[32,2560]{1,0:T(8,128)(2,1)S(1)}, bf16[32,2560]{1,0:T(8,128)(2,1)S(1)}, u32[]{:S(2)}, u32[]{:S(2)}) collective-permute-start(bf16[32,2560]{1,0:T(8,128)(2,1)S(1)} %bitcast.195), channel_id=1, source_target_pairs={{0,16},{1,17},{2,18},{3,19},{4,20},{5,21},{6,22},{7,23},{8,24},{9,... | collective-permute-start | bytes 491528 | tf_op jit(solution)/shard_map/ppermute | solution.py:29
  17.7 8.5 %collective-permute-start.3 = (bf16[32,2560]{1,0:T(8,128)(2,1)S(1)}, bf16[32,2560]{1,0:T(8,128)(2,1)S(1)}, u32[]{:S(2)}, u32[]{:S(2)}) collective-permute-start(bf16[32,2560]{1,0:T(8,128)(2,1)S(1)} %bitcast.196), channel_id=1, source_target_pairs={{0,24},{1,25},{2,26},{3,27},{4,28},{5,29},{6,30},{7,31},{8,0},{9,1... | collective-permute-start | bytes 491528 | tf_op jit(solution)/shard_map/ppermute | solution.py:29
  19.1 10.7 %collective-permute-start.12 = (bf16[32,2688]{1,0:T(8,128)(2,1)S(1)}, bf16[32,2688]{1,0:T(8,128)(2,1)S(1)}, u32[]{:S(2)}, u32[]{:S(2)}) collective-permute-start(bf16[32,2688]{1,0:T(8,128)(2,1)S(1)} %bitcast.190), channel_id=1, source_target_pairs={{0,2},{1,3},{2,4},{3,5},{4,6},{5,7},{6,0},{7,1},{8,10},{9,11},{10,... | collective-permute-start | bytes 516104 | tf_op jit(solution)/shard_map/ppermute | solution.py:29
  21.0 12.1 %collective-permute-start.11 = (bf16[32,2688]{1,0:T(8,128)(2,1)S(1)}, bf16[32,2688]{1,0:T(8,128)(2,1)S(1)}, u32[]{:S(2)}, u32[]{:S(2)}) collective-permute-start(bf16[32,2688]{1,0:T(8,128)(2,1)S(1)} %bitcast.191), channel_id=1, source_target_pairs={{0,4},{1,5},{2,6},{3,7},{4,0},{5,1},{6,2},{7,3},{8,12},{9,13},{10,... | collective-permute-start | bytes 516104 | tf_op jit(solution)/shard_map/ppermute | solution.py:29
  25.3 18.7 %collective-permute-start.10 = (bf16[32,2688]{1,0:T(8,128)(2,1)S(1)}, bf16[32,2688]{1,0:T(8,128)(2,1)S(1)}, u32[]{:S(2)}, u32[]{:S(2)}) collective-permute-start(bf16[32,2688]{1,0:T(8,128)(2,1)S(1)} %bitcast.192), channel_id=1, source_target_pairs={{0,6},{1,7},{2,0},{3,1},{4,2},{5,3},{6,4},{7,5},{8,14},{9,15},{10,... | collective-permute-start | bytes 516104 | tf_op jit(solution)/shard_map/ppermute | solution.py:29
  26.3 23.0 %collective-permute-start.8 = (bf16[128,2560]{1,0:T(8,128)(2,1)S(1)}, bf16[128,2560]{1,0:T(8,128)(2,1)S(1)}, u32[]{:S(2)}, u32[]{:S(2)}) collective-permute-start(bf16[128,2560]{1,0:T(8,128)(2,1)S(1)} %pad_maximum_fusion.2), channel_id=1, source_target_pairs={{0,2},{1,3},{2,4},{3,5},{4,6},{5,7},{6,0},{7,1},{8,10},{9,11},{10,... | collective-permute-start | bytes 1966088 | tf_op jit(solution)/shard_map/ppermute | solution.py:29
  27.4 31.3 %collective-permute-start.7 = (bf16[128,2560]{1,0:T(8,128)(2,1)S(1)}, bf16[128,2560]{1,0:T(8,128)(2,1)S(1)}, u32[]{:S(2)}, u32[]{:S(2)}) collective-permute-start(bf16[128,2560]{1,0:T(8,128)(2,1)S(1)} %pad_maximum_fusion.2), channel_id=1, source_target_pairs={{0,4},{1,5},{2,6},{3,7},{4,0},{5,1},{6,2},{7,3},{8,12},{9,13},{10,... | collective-permute-start | bytes 1966088 | tf_op jit(solution)/shard_map/ppermute | solution.py:29
  29.8 29.1 %collective-permute-start.6 = (bf16[128,2560]{1,0:T(8,128)(2,1)S(1)}, bf16[128,2560]{1,0:T(8,128)(2,1)S(1)}, u32[]{:S(2)}, u32[]{:S(2)}) collective-permute-start(bf16[128,2560]{1,0:T(8,128)(2,1)S(1)} %pad_maximum_fusion.2), channel_id=1, source_target_pairs={{0,6},{1,7},{2,0},{3,1},{4,2},{5,3},{6,4},{7,5},{8,14},{9,15},{10,... | collective-permute-start | bytes 1966088 | tf_op jit(solution)/shard_map/ppermute | solution.py:29
  44.0 26.2 %collective-permute-start.15 = (bf16[128,2688]{1,0:T(8,128)(2,1)S(1)}, bf16[128,2688]{1,0:T(8,128)(2,1)S(1)}, u32[]{:S(2)}, u32[]{:S(2)}) collective-permute-start(bf16[128,2688]{1,0:T(8,128)(2,1)S(1)} %pad_maximum_fusion.1), channel_id=1, source_target_pairs={{0,8},{1,9},{2,10},{3,11},{4,12},{5,13},{6,14},{7,15},{8,16},{9,17... | collective-permute-start | bytes 2064392 | tf_op jit(solution)/shard_map/ppermute | solution.py:29
  44.1 24.3 %collective-permute-start.13 = (bf16[128,2688]{1,0:T(8,128)(2,1)S(1)}, bf16[128,2688]{1,0:T(8,128)(2,1)S(1)}, u32[]{:S(2)}, u32[]{:S(2)}) collective-permute-start(bf16[128,2688]{1,0:T(8,128)(2,1)S(1)} %pad_maximum_fusion.1), channel_id=1, source_target_pairs={{0,24},{1,25},{2,26},{3,27},{4,28},{5,29},{6,30},{7,31},{8,0},{9,1... | collective-permute-start | bytes 2064392 | tf_op jit(solution)/shard_map/ppermute | solution.py:29
  49.4 19.9 %collective-permute-start.14 = (bf16[128,2688]{1,0:T(8,128)(2,1)S(1)}, bf16[128,2688]{1,0:T(8,128)(2,1)S(1)}, u32[]{:S(2)}, u32[]{:S(2)}) collective-permute-start(bf16[128,2688]{1,0:T(8,128)(2,1)S(1)} %pad_maximum_fusion.1), channel_id=1, source_target_pairs={{0,16},{1,17},{2,18},{3,19},{4,20},{5,21},{6,22},{7,23},{8,24},{9,... | collective-permute-start | bytes 2064392 | tf_op jit(solution)/shard_map/ppermute | solution.py:29
  60.8 52.8 %collective-permute-start.9 = (bf16[512,2560]{1,0:T(8,128)(2,1)}, bf16[512,2560]{1,0:T(8,128)(2,1)}, u32[]{:S(2)}, u32[]{:S(2)}) collective-permute-start(bf16[512,2560]{1,0:T(8,128)(2,1)} %bitcast.18.own.own1.own2), channel_id=1, source_target_pairs={{0,1},{1,0},{2,3},{3,2},{4,5},{5,4},{6,7},{7,6},{8,9},{9,8},{10,11... | collective-permute-start | bytes 7864328 | tf_op jit(solution)/shard_map/ppermute | solution.py:29
  71.1 79.6 %collective-permute-start.16 = (bf16[512,2688]{1,0:T(8,128)(2,1)}, bf16[512,2688]{1,0:T(8,128)(2,1)}, u32[]{:S(2)}, u32[]{:S(2)}) collective-permute-start(bf16[512,2688]{1,0:T(8,128)(2,1)} %constant_dynamic-update-slice_fusion.own.dig_own), channel_id=1, source_target_pairs={{0,1},{1,0},{2,3},{3,2},{4,5},{5,4},{6,7},{7,6},{8,9},{9,8},{10,11... | collective-permute-start | bytes 8257544 | tf_op jit(solution)/shard_map/ppermute | solution.py:29
  73.7 39.8 %collective-permute-start.19 = (bf16[1280,640]{1,0:T(8,128)(2,1)}, bf16[1280,640]{1,0:T(8,128)(2,1)}, u32[]{:S(2)}, u32[]{:S(2)}) collective-permute-start(bf16[1280,640]{1,0:T(8,128)(2,1)} %pack.7), channel_id=1, source_target_pairs={{0,32},{32,64},{64,96},{96,0},{1,33},{33,65},{65,97},{97,1},{2,34}... | collective-permute-start | bytes 4915208 | tf_op jit(solution)/shard_map/ppermute | solution.py:17
  77.4 73.2 %collective-permute-start.18 = (bf16[1280,640]{1,0:T(8,128)(2,1)}, bf16[1280,640]{1,0:T(8,128)(2,1)}, u32[]{:S(2)}, u32[]{:S(2)}) collective-permute-start(bf16[1280,640]{1,0:T(8,128)(2,1)} %pack.5), channel_id=1, source_target_pairs={{0,96},{32,0},{64,32},{96,64},{1,97},{33,1},{65,33},{97,65},{2,98}... | collective-permute-start | bytes 4915208 | tf_op jit(solution)/shard_map/ppermute | solution.py:17
  82.3 72.7 %collective-permute-start.17 = (bf16[1280,640]{1,0:T(8,128)(2,1)}, bf16[1280,640]{1,0:T(8,128)(2,1)}, u32[]{:S(2)}, u32[]{:S(2)}) collective-permute-start(bf16[1280,640]{1,0:T(8,128)(2,1)} %pack.4), channel_id=1, source_target_pairs={{0,64},{32,96},{64,0},{96,32},{1,65},{33,97},{65,1},{97,33},{2,66}... | collective-permute-start | bytes 4915208 | tf_op jit(solution)/shard_map/ppermute | solution.py:17
  165.8 23.3 %all-to-all-start = ((f32[32,3,8,128]{3,2,1,0:T(8,128)}), f32[32,3,8,128]{3,2,1,0:T(8,128)}, u32[]{:S(2)}, u32[]{:S(2)}) async-start(f32[32,3,8,128]{3,2,1,0:T(8,128)} %broadcast_in_dim.21), calls=%async_computation | async-start | bytes 786432 | tf_op jit(solution)/shard_map/all_to_all | solution.py:490
  192.0 5.6 %collective-permute-start.25 = (f32[4,8,128]{2,1,0:T(8,128)S(1)}, f32[4,8,128]{2,1,0:T(8,128)S(1)}, u32[]{:S(2)}, u32[]{:S(2)}) collective-permute-start(f32[4,8,128]{2,1,0:T(8,128)S(1)} %get-tuple-element.53), channel_id=1, source_target_pairs={{0,64},{32,96},{64,0},{96,32},{1,65},{33,97},{65,1},{97,33},{2,66}... | collective-permute-start | bytes 49160 | tf_op jit(solution)/shard_map/ppermute | solution.py:17
  192.1 5.7 %collective-permute-start.24 = (f32[4,8,128]{2,1,0:T(8,128)S(1)}, f32[4,8,128]{2,1,0:T(8,128)S(1)}, u32[]{:S(2)}, u32[]{:S(2)}) collective-permute-start(f32[4,8,128]{2,1,0:T(8,128)S(1)} %get-tuple-element.53), channel_id=1, source_target_pairs={{0,96},{32,0},{64,32},{96,64},{1,97},{33,1},{65,33},{97,65},{2,98}... | collective-permute-start | bytes 49160 | tf_op jit(solution)/shard_map/ppermute | solution.py:17
  192.2 5.7 %collective-permute-start.26 = (f32[4,8,128]{2,1,0:T(8,128)S(1)}, f32[4,8,128]{2,1,0:T(8,128)S(1)}, u32[]{:S(2)}, u32[]{:S(2)}) collective-permute-start(f32[4,8,128]{2,1,0:T(8,128)S(1)} %get-tuple-element.53), channel_id=1, source_target_pairs={{0,32},{32,64},{64,96},{96,0},{1,33},{33,65},{65,97},{97,1},{2,34}... | collective-permute-start | bytes 49160 | tf_op jit(solution)/shard_map/ppermute | solution.py:17
  194.4 19.0 %collective-permute-start.21 = (bf16[512,640]{1,0:T(8,128)(2,1)}, bf16[512,640]{1,0:T(8,128)(2,1)S(1)}, u32[]{:S(2)}, u32[]{:S(2)}) collective-permute-start(bf16[512,640]{1,0:T(8,128)(2,1)} %copy-done.11), channel_id=1, source_target_pairs={{0,32},{32,64},{64,96},{96,0},{1,33},{33,65},{65,97},{97,1},{2,34}... | collective-permute-start | bytes 1966088 | tf_op jit(solution)/shard_map/ppermute | solution.py:17
  195.8 19.4 %collective-permute-start.20 = (bf16[512,640]{1,0:T(8,128)(2,1)}, bf16[512,640]{1,0:T(8,128)(2,1)S(1)}, u32[]{:S(2)}, u32[]{:S(2)}) collective-permute-start(bf16[512,640]{1,0:T(8,128)(2,1)} %copy-done.11), channel_id=1, source_target_pairs={{0,96},{32,0},{64,32},{96,64},{1,97},{33,1},{65,33},{97,65},{2,98}... | collective-permute-start | bytes 1966088 | tf_op jit(solution)/shard_map/ppermute | solution.py:17
  197.6 58.1 %collective-permute-start.28 = (bf16[512,640]{1,0:T(8,128)(2,1)}, bf16[512,640]{1,0:T(8,128)(2,1)}, u32[]{:S(2)}, u32[]{:S(2)}) collective-permute-start(bf16[512,640]{1,0:T(8,128)(2,1)} %get-tuple-element.21.own), channel_id=1, source_target_pairs={{0,32},{32,64},{64,96},{96,0},{1,33},{33,65},{65,97},{97,1},{2,34}... | collective-permute-start | bytes 1966088 | tf_op jit(solution)/shard_map/ppermute | solution.py:17
  215.0 18.6 %collective-permute-start.22 = (bf16[256,640]{1,0:T(8,128)(2,1)}, bf16[256,640]{1,0:T(8,128)(2,1)}, u32[]{:S(2)}, u32[]{:S(2)}) collective-permute-start(bf16[256,640]{1,0:T(8,128)(2,1)} %slice.158), channel_id=1, source_target_pairs={{0,32},{32,64},{64,96},{96,0},{1,33},{33,65},{65,97},{97,1},{2,34}... | collective-permute-start | bytes 983048 | tf_op jit(solution)/shard_map/ppermute | solution.py:17
  216.8 16.8 %collective-permute-start.23 = (bf16[256,640]{1,0:T(8,128)(2,1)}, bf16[256,640]{1,0:T(8,128)(2,1)}, u32[]{:S(2)}, u32[]{:S(2)}) collective-permute-start(bf16[256,640]{1,0:T(8,128)(2,1)} %slice.159), channel_id=1, source_target_pairs={{0,96},{32,0},{64,32},{96,64},{1,97},{33,1},{65,33},{97,65},{2,98}... | collective-permute-start | bytes 983048 | tf_op jit(solution)/shard_map/ppermute | solution.py:17
  250.7 31.5 %collective-permute-start.31 = (f32[256,1280]{1,0:T(8,128)}, f32[256,1280]{1,0:T(8,128)}, u32[]{:S(2)}, u32[]{:S(2)}) collective-permute-start(f32[256,1280]{1,0:T(8,128)} %get-tuple-element.23), channel_id=1, source_target_pairs={{0,1},{1,0},{2,3},{3,2},{4,5},{5,4},{6,7},{7,6},{8,9},{9,8},{10,11... | collective-permute-start | bytes 3932168 | tf_op jit(solution)/shard_map/ppermute | solution.py:29
  250.8 18.0 %collective-permute-start.27 = (bf16[512,640]{1,0:T(8,128)(2,1)}, bf16[512,640]{1,0:T(8,128)(2,1)}, u32[]{:S(2)}, u32[]{:S(2)}) collective-permute-start(bf16[512,640]{1,0:T(8,128)(2,1)} %get-tuple-element.21.own), channel_id=1, source_target_pairs={{0,96},{32,0},{64,32},{96,64},{1,97},{33,1},{65,33},{97,65},{2,98}... | collective-permute-start | bytes 1966088 | tf_op jit(solution)/shard_map/ppermute | solution.py:17
  252.4 17.6 %collective-permute-start.34 = (bf16[16,1280]{1,0:T(8,128)(2,1)S(1)}, bf16[16,1280]{1,0:T(8,128)(2,1)S(1)}, u32[]{:S(2)}, u32[]{:S(2)}) collective-permute-start(bf16[16,1280]{1,0:T(8,128)(2,1)S(1)} %get-tuple-element.47), channel_id=1, source_target_pairs={{0,32},{32,64},{64,96},{96,0},{1,33},{33,65},{65,97},{97,1},{2,34}... | collective-permute-start | bytes 122888 | tf_op jit(solution)/shard_map/ppermute | solution.py:17
  253.5 19.6 %collective-permute-start.33 = (bf16[16,1280]{1,0:T(8,128)(2,1)S(1)}, bf16[16,1280]{1,0:T(8,128)(2,1)S(1)}, u32[]{:S(2)}, u32[]{:S(2)}) collective-permute-start(bf16[16,1280]{1,0:T(8,128)(2,1)S(1)} %get-tuple-element.48), channel_id=1, source_target_pairs={{0,64},{32,96},{64,0},{96,32},{1,65},{33,97},{65,1},{97,33},{2,66}... | collective-permute-start | bytes 122888 | tf_op jit(solution)/shard_map/ppermute | solution.py:17
  255.7 17.5 %collective-permute-start.32 = (bf16[16,1280]{1,0:T(8,128)(2,1)S(1)}, bf16[16,1280]{1,0:T(8,128)(2,1)S(1)}, u32[]{:S(2)}, u32[]{:S(2)}) collective-permute-start(bf16[16,1280]{1,0:T(8,128)(2,1)S(1)} %get-tuple-element.49), channel_id=1, source_target_pairs={{0,96},{32,0},{64,32},{96,64},{1,97},{33,1},{65,33},{97,65},{2,98}... | collective-permute-start | bytes 122888 | tf_op jit(solution)/shard_map/ppermute | solution.py:17
  268.8 14.9 %collective-permute-start.29 = (bf16[256,640]{1,0:T(8,128)(2,1)S(1)}, bf16[256,640]{1,0:T(8,128)(2,1)S(1)}, u32[]{:S(2)}, u32[]{:S(2)}) collective-permute-start(bf16[256,640]{1,0:T(8,128)(2,1)S(1)} %slice.168), channel_id=1, source_target_pairs={{0,32},{32,64},{64,96},{96,0},{1,33},{33,65},{65,97},{97,1},{2,34}... | collective-permute-start | bytes 983048 | tf_op jit(solution)/shard_map/ppermute | solution.py:17
  270.0 13.8 %collective-permute-start.30 = (bf16[256,640]{1,0:T(8,128)(2,1)S(1)}, bf16[256,640]{1,0:T(8,128)(2,1)S(1)}, u32[]{:S(2)}, u32[]{:S(2)}) collective-permute-start(bf16[256,640]{1,0:T(8,128)(2,1)S(1)} %slice.169), channel_id=1, source_target_pairs={{0,96},{32,0},{64,32},{96,64},{1,97},{33,1},{65,33},{97,65},{2,98}... | collective-permute-start | bytes 983048 | tf_op jit(solution)/shard_map/ppermute | solution.py:17
  292.1 19.3 %collective-permute-start.41 = (f32[256,1280]{1,0:T(8,128)S(1)}, f32[256,1280]{1,0:T(8,128)S(1)}, u32[]{:S(2)}, u32[]{:S(2)}) collective-permute-start(f32[256,1280]{1,0:T(8,128)S(1)} %get-tuple-element.28), channel_id=1, source_target_pairs={{0,1},{1,0},{2,3},{3,2},{4,5},{5,4},{6,7},{7,6},{8,9},{9,8},{10,11... | collective-permute-start | bytes 3932168 | tf_op jit(solution)/shard_map/ppermute | solution.py:29
  292.3 18.4 %collective-permute-start.35 = (f32[2,4,8,1280]{3,2,1,0:T(8,128)S(1)}, f32[2,4,8,1280]{3,2,1,0:T(8,128)S(1)}, u32[]{:S(2)}, u32[]{:S(2)}) collective-permute-start(f32[2,4,8,1280]{3,2,1,0:T(8,128)S(1)} %get-tuple-element.32), channel_id=1, source_target_pairs={{0,8},{1,9},{2,10},{3,11},{4,12},{5,13},{6,14},{7,15},{8,16},{9,17... | collective-permute-start | bytes 983048 | tf_op jit(solution)/shard_map/ppermute | solution.py:29
  292.8 17.9 %collective-permute-start.37 = (f32[2,4,8,1280]{3,2,1,0:T(8,128)S(1)}, f32[2,4,8,1280]{3,2,1,0:T(8,128)S(1)}, u32[]{:S(2)}, u32[]{:S(2)}) collective-permute-start(f32[2,4,8,1280]{3,2,1,0:T(8,128)S(1)} %get-tuple-element.33), channel_id=1, source_target_pairs={{0,16},{1,17},{2,18},{3,19},{4,20},{5,21},{6,22},{7,23},{8,24},{9,... | collective-permute-start | bytes 983048 | tf_op jit(solution)/shard_map/ppermute | solution.py:29
  294.8 16.5 %collective-permute-start.36 = (f32[2,4,8,1280]{3,2,1,0:T(8,128)S(1)}, f32[2,4,8,1280]{3,2,1,0:T(8,128)S(1)}, u32[]{:S(2)}, u32[]{:S(2)}) collective-permute-start(f32[2,4,8,1280]{3,2,1,0:T(8,128)S(1)} %get-tuple-element.34), channel_id=1, source_target_pairs={{0,24},{1,25},{2,26},{3,27},{4,28},{5,29},{6,30},{7,31},{8,0},{9,1... | collective-permute-start | bytes 983048 | tf_op jit(solution)/shard_map/ppermute | solution.py:29
  311.6 10.6 %collective-permute-start.42 = (f32[2,4,8,1280]{3,2,1,0:T(8,128)S(1)}, f32[2,4,8,1280]{3,2,1,0:T(8,128)S(1)}, u32[]{:S(2)}, u32[]{:S(2)}) collective-permute-start(f32[2,4,8,1280]{3,2,1,0:T(8,128)S(1)} %get-tuple-element.35), channel_id=1, source_target_pairs={{0,8},{1,9},{2,10},{3,11},{4,12},{5,13},{6,14},{7,15},{8,16},{9,17... | collective-permute-start | bytes 983048 | tf_op jit(solution)/shard_map/ppermute | solution.py:29
  312.4 18.0 %collective-permute-start.44 = (f32[2,4,8,1280]{3,2,1,0:T(8,128)S(1)}, f32[2,4,8,1280]{3,2,1,0:T(8,128)S(1)}, u32[]{:S(2)}, u32[]{:S(2)}) collective-permute-start(f32[2,4,8,1280]{3,2,1,0:T(8,128)S(1)} %get-tuple-element.36), channel_id=1, source_target_pairs={{0,16},{1,17},{2,18},{3,19},{4,20},{5,21},{6,22},{7,23},{8,24},{9,... | collective-permute-start | bytes 983048 | tf_op jit(solution)/shard_map/ppermute | solution.py:29
  315.8 14.6 %collective-permute-start.43 = (f32[2,4,8,1280]{3,2,1,0:T(8,128)S(1)}, f32[2,4,8,1280]{3,2,1,0:T(8,128)S(1)}, u32[]{:S(2)}, u32[]{:S(2)}) collective-permute-start(f32[2,4,8,1280]{3,2,1,0:T(8,128)S(1)} %get-tuple-element.37), channel_id=1, source_target_pairs={{0,24},{1,25},{2,26},{3,27},{4,28},{5,29},{6,30},{7,31},{8,0},{9,1... | collective-permute-start | bytes 983048 | tf_op jit(solution)/shard_map/ppermute | solution.py:29
  315.8 17.3 %collective-permute-start.38 = (f32[2,8,1280]{2,1,0:T(8,128)S(1)}, f32[2,8,1280]{2,1,0:T(8,128)S(1)}, u32[]{:S(2)}, u32[]{:S(2)}) collective-permute-start(f32[2,8,1280]{2,1,0:T(8,128)S(1)} %get-tuple-element.40), channel_id=1, source_target_pairs={{0,2},{1,3},{2,4},{3,5},{4,6},{5,7},{6,0},{7,1},{8,10},{9,11},{10,... | collective-permute-start | bytes 245768 | tf_op jit(solution)/shard_map/ppermute | solution.py:29
  316.3 17.7 %collective-permute-start.40 = (f32[2,8,1280]{2,1,0:T(8,128)S(1)}, f32[2,8,1280]{2,1,0:T(8,128)S(1)}, u32[]{:S(2)}, u32[]{:S(2)}) collective-permute-start(f32[2,8,1280]{2,1,0:T(8,128)S(1)} %get-tuple-element.41), channel_id=1, source_target_pairs={{0,4},{1,5},{2,6},{3,7},{4,0},{5,1},{6,2},{7,3},{8,12},{9,13},{10,... | collective-permute-start | bytes 245768 | tf_op jit(solution)/shard_map/ppermute | solution.py:29
  322.2 11.9 %collective-permute-start.39 = (f32[2,8,1280]{2,1,0:T(8,128)S(1)}, f32[2,8,1280]{2,1,0:T(8,128)S(1)}, u32[]{:S(2)}, u32[]{:S(2)}) collective-permute-start(f32[2,8,1280]{2,1,0:T(8,128)S(1)} %get-tuple-element.42), channel_id=1, source_target_pairs={{0,6},{1,7},{2,0},{3,1},{4,2},{5,3},{6,4},{7,5},{8,14},{9,15},{10,... | collective-permute-start | bytes 245768 | tf_op jit(solution)/shard_map/ppermute | solution.py:29
  330.5 6.6 %collective-permute-start.45 = (f32[2,8,1280]{2,1,0:T(8,128)S(1)}, f32[2,8,1280]{2,1,0:T(8,128)S(1)}, u32[]{:S(2)}, u32[]{:S(2)}) collective-permute-start(f32[2,8,1280]{2,1,0:T(8,128)S(1)} %get-tuple-element.43), channel_id=1, source_target_pairs={{0,2},{1,3},{2,4},{3,5},{4,6},{5,7},{6,0},{7,1},{8,10},{9,11},{10,... | collective-permute-start | bytes 245768 | tf_op jit(solution)/shard_map/ppermute | solution.py:29
  331.0 6.1 %collective-permute-start.47 = (f32[2,8,1280]{2,1,0:T(8,128)S(1)}, f32[2,8,1280]{2,1,0:T(8,128)S(1)}, u32[]{:S(2)}, u32[]{:S(2)}) collective-permute-start(f32[2,8,1280]{2,1,0:T(8,128)S(1)} %get-tuple-element.44), channel_id=1, source_target_pairs={{0,4},{1,5},{2,6},{3,7},{4,0},{5,1},{6,2},{7,3},{8,12},{9,13},{10,... | collective-permute-start | bytes 245768 | tf_op jit(solution)/shard_map/ppermute | solution.py:29
  333.1 4.9 %collective-permute-start.46 = (f32[2,8,1280]{2,1,0:T(8,128)S(1)}, f32[2,8,1280]{2,1,0:T(8,128)S(1)}, u32[]{:S(2)}, u32[]{:S(2)}) collective-permute-start(f32[2,8,1280]{2,1,0:T(8,128)S(1)} %get-tuple-element.45), channel_id=1, source_target_pairs={{0,6},{1,7},{2,0},{3,1},{4,2},{5,3},{6,4},{7,5},{8,14},{9,15},{10,... | collective-permute-start | bytes 245768 | tf_op jit(solution)/shard_map/ppermute | solution.py:29
  (18 other events, 329.8 us)
